TPU v7x, 1024 devices: a whole 8x8x8 slice. The times are simulated.
1024 devices in a mesh: gx: 16 (over x, y_hi), gy: 8 (over z), gz: 8 (over y_lo, core).
Axes of the slice: x: 8, y: 8 (y_hi: 2, y_lo: 4; y = y_hi * 4 + y_lo), z: 8, core: 2. Of those that a mesh axis runs over, the one named last changes fastest.
Arguments:
- density_scatter: float32 [64, 64, 1024], P('gx', 'gy', 'gz'), may hold values from 0.8 to 1.25
- initial_velocity: float32 [3, 64, 64, 1024], P(None, 'gx', 'gy', 'gz'), may hold values from -0.12 to 0.12
- bubble_mask: int32 [64, 64, 1024], P('gx', 'gy', 'gz'), may hold values from 0 to 1, as said below
- wall_flags: int32 [64, 64, 1024], P('gx', 'gy', 'gz'), may hold values 0 or 1
Outputs:
- density_field: float32 [64, 64, 1024], P('gx', 'gy', 'gz')
- velocity_field: float32 [3, 64, 64, 1024], P(None, 'gx', 'gy', 'gz')
Inputs may be any that keep to these rules, and one draw needn't show every extreme that they name: `bubble_mask`: 1 at nodes inside a vapour bubble, 0 in the liquid. `wall_flags`: 1 at solid nodes, 0 at fluid nodes.
All inputs are finite; a program needn't handle non-finite values. No bound on the sum of `wall_flags` on one device may be relied on, other than what follows from the above.
Results may differ from a plain program's by a relative error of at most 0.0003.
Values sent between devices are 32-bit elements; how exact they have to be, the bound alone decides.
A program may use at most 32 MiB of HBM per device.

v0:
```python
import math

import jax
import jax.numpy as jnp
import numpy as np
from jax import lax
from jax.sharding import PartitionSpec as P

STEPS = 4


lattice_velocities = np.array(
    [
        [0, 0, 0],
        [1, 0, 0],
        [-1, 0, 0],
        [0, 1, 0],
        [0, -1, 0],
        [0, 0, 1],
        [0, 0, -1],
        [1, 1, 0],
        [-1, -1, 0],
        [1, -1, 0],
        [-1, 1, 0],
        [1, 0, 1],
        [-1, 0, -1],
        [1, 0, -1],
        [-1, 0, 1],
        [0, 1, 1],
        [0, -1, -1],
        [0, 1, -1],
        [0, -1, 1],
    ]
)
weights = [1.0 / 3.0] + [1.0 / 18.0] * 6 + [1.0 / 36.0] * 12
opposite = [0, 2, 1, 4, 3, 6, 5, 8, 7, 10, 9, 12, 11, 14, 13, 16, 15, 18, 17]
liquid = 0.28
vapour = 0.06
wall_potential = 0.5
attractive_coupling = 1.0
critical_thermal_ratio = 0.06
viscous_rate = 1.25


def extended(shard, sides, width):
    for axis, dim in sides:
        peers, length = (lax.axis_size(axis), shard.shape[dim])
        up = [(i, (i + 1) % peers) for i in range(peers)]
        down = [(j, i) for i, j in up]
        last = lax.slice_in_dim(shard, length - width, length, axis=dim)
        first = lax.slice_in_dim(shard, 0, width, axis=dim)
        before = lax.ppermute(last, axis, up)
        after = lax.ppermute(first, axis, down)
        shard = jnp.concatenate([before, shard, after], axis=dim)
    return shard


def relaxation_matrix():
    table = lattice_velocities * 1.0
    first, second, third = (table[:, 0], table[:, 1], table[:, 2])
    squared_speed = first * first + second * second + third * third
    rows = [
        np.ones(19),
        19.0 * squared_speed - 30.0,
        (21.0 * squared_speed * squared_speed - 53.0 * squared_speed + 24.0) / 2.0,
        first,
        (5.0 * squared_speed - 9.0) * first,
        second,
        (5.0 * squared_speed - 9.0) * second,
        third,
        (5.0 * squared_speed - 9.0) * third,
        3.0 * first * first - squared_speed,
        (3.0 * squared_speed - 5.0) * (3.0 * first * first - squared_speed),
        second * second - third * third,
        (3.0 * squared_speed - 5.0) * (second * second - third * third),
        first * second,
        second * third,
        first * third,
        first * (second * second - third * third),
        second * (third * third - first * first),
        third * (first * first - second * second),
    ]
    moment_space_vector = np.stack(rows)
    inverse_transform = moment_space_vector.T / np.sum(
        moment_space_vector * moment_space_vector, axis=1
    )
    rates = np.array(
        [
            0.0,
            1.19,
            1.4,
            0.0,
            1.2,
            0.0,
            1.2,
            0.0,
            1.2,
            viscous_rate,
            1.4,
            viscous_rate,
            1.4,
            viscous_rate,
            viscous_rate,
            viscous_rate,
            1.98,
            1.98,
            1.98,
        ]
    )
    return inverse_transform * rates[None, :] @ moment_space_vector


def equilibrium(mass_per_volume, velocity):
    squared_speed = (
        velocity[0] * velocity[0] + velocity[1] * velocity[1] + velocity[2] * velocity[2]
    )
    rows = []
    for i in range(19):
        projection = (
            float(lattice_velocities[i, 0]) * velocity[0]
            + float(lattice_velocities[i, 1]) * velocity[1]
            + float(lattice_velocities[i, 2]) * velocity[2]
        )
        rows.append(
            weights[i]
            * mass_per_volume
            * (1.0 + 3.0 * projection + 4.5 * projection * projection - 1.5 * squared_speed)
        )
    return jnp.stack(rows)


def moments(populations):
    return jnp.stack(
        [
            sum(
                (
                    float(lattice_velocities[i, k]) * populations[i]
                    for i in range(19)
                    if lattice_velocities[i, k] != 0
                )
            )
            for k in range(3)
        ]
    )


def pseudo_potential(mass_per_volume):
    thermodynamic_stress = (
        mass_per_volume
        * critical_thermal_ratio
        * (
            1.0
            + mass_per_volume
            + mass_per_volume * mass_per_volume
            - mass_per_volume * mass_per_volume * mass_per_volume
        )
        / ((1.0 - mass_per_volume) * (1.0 - mass_per_volume) * (1.0 - mass_per_volume))
        - attractive_coupling * mass_per_volume * mass_per_volume
    )
    return jnp.sqrt(6.0 * (mass_per_volume / 3.0 - thermodynamic_stress))


def attraction(potential, nearby):
    parts = []
    for k in range(3):
        total = sum(
            (
                weights[i] * float(lattice_velocities[i, k]) * nearby[i - 1]
                for i in range(1, 19)
                if lattice_velocities[i, k] != 0
            )
        )
        parts.append(potential * total)
    return jnp.stack(parts)


def collide(populations, mass_per_volume, momentum, force, solid, kernel):
    velocity = momentum / mass_per_volume
    settled = equilibrium(mass_per_volume, velocity)
    pushed = equilibrium(mass_per_volume, velocity + force / mass_per_volume)
    relaxed = jnp.einsum(
        "ij,jxyz->ixyz", kernel, populations - settled, precision=lax.Precision.HIGHEST
    )
    relaxed_distribution = populations - relaxed + pushed - settled
    bounced = populations[np.array(opposite)]
    return jnp.where(solid[None], bounced, relaxed_distribution)


def window(padded, offsets, shape):
    starts = [1 + int(offsets[k]) for k in range(3)]
    return lax.slice(padded, starts, [starts[k] + shape[k] for k in range(3)])


def on_device(density_scatter, initial_velocity, bubble_mask, wall_flags):
    kernel = jnp.asarray(relaxation_matrix(), jnp.float32)
    solid = wall_flags == 1
    shape = wall_flags.shape
    mass_per_volume = jnp.where(bubble_mask == 1, vapour, liquid) * density_scatter
    populations = equilibrium(mass_per_volume, initial_velocity)
    for step in range(STEPS):
        mass_per_volume = jnp.sum(populations, axis=0)
        momentum = moments(populations)
        potential = jnp.where(solid, wall_potential, pseudo_potential(mass_per_volume))
        padded = extended(potential, (("gx", 0), ("gy", 1), ("gz", 2)), 1)
        nearby = [window(padded, lattice_velocities[i], shape) for i in range(1, 19)]
        force = attraction(potential, nearby)
        post = collide(populations, mass_per_volume, momentum, force, solid, kernel)
        widened_field = extended(post, (("gx", 1), ("gy", 2), ("gz", 3)), 1)
        populations = jnp.stack(
            [window(widened_field[i], -lattice_velocities[i], shape) for i in range(19)]
        )
    mass_per_volume = jnp.sum(populations, axis=0)
    momentum = moments(populations)
    density_field = jnp.where(solid, 0.0, mass_per_volume / liquid)
    velocity_field = jnp.where(solid[None], 0.0, math.sqrt(3.0) * momentum / mass_per_volume)
    return (density_field, velocity_field)


def solution(mesh):
    in_specs = (
        P("gx", "gy", "gz"),
        P(None, "gx", "gy", "gz"),
        P("gx", "gy", "gz"),
        P("gx", "gy", "gz"),
    )
    out_specs = (P("gx", "gy", "gz"), P(None, "gx", "gy", "gz"))
    return jax.shard_map(
        on_device, mesh=mesh, in_specs=in_specs, out_specs=out_specs, check_vma=False
    )
```

profile of v0, /device:TPU:1, one launch (start us, length us, event | category | flops | bytes accessed | tf_op | source)
XLA Modules:
  0.0 317.9 jit_solution(7987287609962380325)
XLA Ops:
  1.6 8.7 %collective-permute-start.1 = (f32[1,8,128]{2,1,0:T(8,128)S(1)}, f32[1,8,128]{2,1,0:T(8,128)S(1)}, u32[]{:S(2)}, u32[]{:S(2)}) collective-permute-start(f32[1,8,128]{2,1,0:T(8,128)S(1)} %get-tuple-element.329), channel_id=1, source_target_pairs={{0,64},{64,128},{128,192},{192,256},{256,320},{320,384},{384,448},... | collective-permute-start | bytes 12296 | tf_op jit(solution)/shard_map/ppermute | solution.py:52
  10.3 4.2 %collective-permute-start = (f32[1,8,128]{2,1,0:T(8,128)S(1)}, f32[1,8,128]{2,1,0:T(8,128)S(1)}, u32[]{:S(2)}, u32[]{:S(2)}) collective-permute-start(f32[1,8,128]{2,1,0:T(8,128)S(1)} %get-tuple-element.330), channel_id=1, source_target_pairs={{64,0},{128,64},{192,128},{256,192},{320,256},{384,320},{448,384},... | collective-permute-start | bytes 12296 | tf_op jit(solution)/shard_map/ppermute | solution.py:53
  18.6 4.9 %collective-permute-start.3 = (f32[6,1,128]{2,1,0:T(1,128)S(1)}, f32[6,1,128]{2,1,0:T(1,128)S(1)}, u32[]{:S(2)}, u32[]{:S(2)}) collective-permute-start(f32[6,1,128]{2,1,0:T(1,128)S(1)} %get-tuple-element.181), channel_id=1, source_target_pairs={{0,8},{8,16},{16,24},{24,32},{32,40},{40,48},{48,56},{56,0},{1,9},... | collective-permute-start | bytes 9224 | tf_op jit(solution)/shard_map/ppermute | solution.py:52
  23.5 14.0 %collective-permute-start.2 = (f32[6,1,128]{2,1,0:T(1,128)S(1)}, f32[6,1,128]{2,1,0:T(1,128)S(1)}, u32[]{:S(2)}, u32[]{:S(2)}) collective-permute-start(f32[6,1,128]{2,1,0:T(1,128)S(1)} %get-tuple-element.182), channel_id=1, source_target_pairs={{8,0},{16,8},{24,16},{32,24},{40,32},{48,40},{56,48},{0,56},{9,1},... | collective-permute-start | bytes 9224 | tf_op jit(solution)/shard_map/ppermute | solution.py:53
  38.9 4.3 %collective-permute-start.4 = (f32[6,10,1]{2,1,0:T(8,128)S(1)}, f32[6,10,1]{2,1,0:T(8,128)S(1)}, u32[]{:S(2)}, u32[]{:S(2)}) collective-permute-start(f32[6,10,1]{2,1,0:T(8,128)S(1)} %get-tuple-element.165), channel_id=1, source_target_pairs={{1,0},{2,1},{3,2},{4,3},{5,4},{6,5},{7,6},{0,7},{9,8},{10,9},{11,1... | collective-permute-start | bytes 728 | tf_op jit(solution)/shard_map/ppermute | solution.py:53
  48.8 4.0 %collective-permute-start.6 = (f32[19,1,8,128]{3,2,1,0:T(8,128)S(1)}, f32[19,1,8,128]{3,2,1,0:T(8,128)S(1)}, u32[]{:S(2)}, u32[]{:S(2)}) collective-permute-start(f32[19,1,8,128]{3,2,1,0:T(8,128)S(1)} %get-tuple-element.146), channel_id=1, source_target_pairs={{0,64},{64,128},{128,192},{192,256},{256,320},{320,384},{384,448},... | collective-permute-start | bytes 233480 | tf_op jit(solution)/shard_map/ppermute | solution.py:52
  52.8 7.3 %collective-permute-start.7 = (f32[19,1,8,128]{3,2,1,0:T(8,128)S(1)}, f32[19,1,8,128]{3,2,1,0:T(8,128)S(1)}, u32[]{:S(2)}, u32[]{:S(2)}) collective-permute-start(f32[19,1,8,128]{3,2,1,0:T(8,128)S(1)} %get-tuple-element.147), channel_id=1, source_target_pairs={{64,0},{128,64},{192,128},{256,192},{320,256},{384,320},{448,384},... | collective-permute-start | bytes 233480 | tf_op jit(solution)/shard_map/ppermute | solution.py:53
  64.6 5.1 %collective-permute-start.9 = (f32[19,6,1,128]{3,2,1,0:T(1,128)S(1)}, f32[19,6,1,128]{3,2,1,0:T(1,128)S(1)}, u32[]{:S(2)}, u32[]{:S(2)}) collective-permute-start(f32[19,6,1,128]{3,2,1,0:T(1,128)S(1)} %get-tuple-element.139), channel_id=1, source_target_pairs={{8,0},{16,8},{24,16},{32,24},{40,32},{48,40},{56,48},{0,56},{9,1},... | collective-permute-start | bytes 175112 | tf_op jit(solution)/shard_map/ppermute | solution.py:53
  72.0 7.9 %collective-permute-start.10 = (f32[19,6,10,1]{0,3,2,1:T(1,128)S(1)}, f32[19,6,10,1]{0,3,2,1:T(1,128)S(1)}, u32[]{:S(2)}, u32[]{:S(2)}) collective-permute-start(f32[19,6,10,1]{0,3,2,1:T(1,128)S(1)} %copy.2651), channel_id=1, source_target_pairs={{0,1},{1,2},{2,3},{3,4},{4,5},{5,6},{6,7},{7,0},{8,9},{9,10},{10,1... | collective-permute-start | bytes 13688 | tf_op jit(solution)/shard_map/ppermute | solution.py:52
  88.8 5.7 %collective-permute-start.13 = (f32[1,8,128]{2,1,0:T(8,128)S(1)}, f32[1,8,128]{2,1,0:T(8,128)S(1)}, u32[]{:S(2)}, u32[]{:S(2)}) collective-permute-start(f32[1,8,128]{2,1,0:T(8,128)S(1)} %get-tuple-element.292), channel_id=1, source_target_pairs={{0,64},{64,128},{128,192},{192,256},{256,320},{320,384},{384,448},... | collective-permute-start | bytes 12296 | tf_op jit(solution)/shard_map/ppermute | solution.py:52
  94.5 5.6 %collective-permute-start.12 = (f32[1,8,128]{2,1,0:T(8,128)S(1)}, f32[1,8,128]{2,1,0:T(8,128)S(1)}, u32[]{:S(2)}, u32[]{:S(2)}) collective-permute-start(f32[1,8,128]{2,1,0:T(8,128)S(1)} %get-tuple-element.293), channel_id=1, source_target_pairs={{64,0},{128,64},{192,128},{256,192},{320,256},{384,320},{448,384},... | collective-permute-start | bytes 12296 | tf_op jit(solution)/shard_map/ppermute | solution.py:53
  104.7 5.2 %collective-permute-start.14 = (f32[6,1,128]{2,1,0:T(1,128)S(1)}, f32[6,1,128]{2,1,0:T(1,128)S(1)}, u32[]{:S(2)}, u32[]{:S(2)}) collective-permute-start(f32[6,1,128]{2,1,0:T(1,128)S(1)} %get-tuple-element.178), channel_id=1, source_target_pairs={{8,0},{16,8},{24,16},{32,24},{40,32},{48,40},{56,48},{0,56},{9,1},... | collective-permute-start | bytes 9224 | tf_op jit(solution)/shard_map/ppermute | solution.py:53
  110.7 6.6 %collective-permute-start.16 = (f32[6,10,1]{2,1,0:T(8,128)S(1)}, f32[6,10,1]{2,1,0:T(8,128)S(1)}, u32[]{:S(2)}, u32[]{:S(2)}) collective-permute-start(f32[6,10,1]{2,1,0:T(8,128)S(1)} %get-tuple-element.163), channel_id=1, source_target_pairs={{1,0},{2,1},{3,2},{4,3},{5,4},{6,5},{7,6},{0,7},{9,8},{10,9},{11,1... | collective-permute-start | bytes 728 | tf_op jit(solution)/shard_map/ppermute | solution.py:53
  123.7 4.5 %collective-permute-start.18 = (f32[19,1,8,128]{3,2,1,0:T(8,128)S(1)}, f32[19,1,8,128]{3,2,1,0:T(8,128)S(1)}, u32[]{:S(2)}, u32[]{:S(2)}) collective-permute-start(f32[19,1,8,128]{3,2,1,0:T(8,128)S(1)} %get-tuple-element.144), channel_id=1, source_target_pairs={{0,64},{64,128},{128,192},{192,256},{256,320},{320,384},{384,448},... | collective-permute-start | bytes 233480 | tf_op jit(solution)/shard_map/ppermute | solution.py:52
  128.2 6.8 %collective-permute-start.19 = (f32[19,1,8,128]{3,2,1,0:T(8,128)S(1)}, f32[19,1,8,128]{3,2,1,0:T(8,128)S(1)}, u32[]{:S(2)}, u32[]{:S(2)}) collective-permute-start(f32[19,1,8,128]{3,2,1,0:T(8,128)S(1)} %get-tuple-element.145), channel_id=1, source_target_pairs={{64,0},{128,64},{192,128},{256,192},{320,256},{384,320},{448,384},... | collective-permute-start | bytes 233480 | tf_op jit(solution)/shard_map/ppermute | solution.py:53
  139.2 4.8 %collective-permute-start.21 = (f32[19,6,1,128]{3,2,1,0:T(1,128)S(1)}, f32[19,6,1,128]{3,2,1,0:T(1,128)S(1)}, u32[]{:S(2)}, u32[]{:S(2)}) collective-permute-start(f32[19,6,1,128]{3,2,1,0:T(1,128)S(1)} %get-tuple-element.137), channel_id=1, source_target_pairs={{8,0},{16,8},{24,16},{32,24},{40,32},{48,40},{56,48},{0,56},{9,1},... | collective-permute-start | bytes 175112 | tf_op jit(solution)/shard_map/ppermute | solution.py:53
  146.4 7.6 %collective-permute-start.22 = (f32[19,6,10,1]{0,3,2,1:T(1,128)S(1)}, f32[19,6,10,1]{0,3,2,1:T(1,128)S(1)}, u32[]{:S(2)}, u32[]{:S(2)}) collective-permute-start(f32[19,6,10,1]{0,3,2,1:T(1,128)S(1)} %copy.2695), channel_id=1, source_target_pairs={{0,1},{1,2},{2,3},{3,4},{4,5},{5,6},{6,7},{7,0},{8,9},{9,10},{10,1... | collective-permute-start | bytes 13688 | tf_op jit(solution)/shard_map/ppermute | solution.py:52
  163.1 5.5 %collective-permute-start.25 = (f32[1,8,128]{2,1,0:T(8,128)S(1)}, f32[1,8,128]{2,1,0:T(8,128)S(1)}, u32[]{:S(2)}, u32[]{:S(2)}) collective-permute-start(f32[1,8,128]{2,1,0:T(8,128)S(1)} %get-tuple-element.255), channel_id=1, source_target_pairs={{0,64},{64,128},{128,192},{192,256},{256,320},{320,384},{384,448},... | collective-permute-start | bytes 12296 | tf_op jit(solution)/shard_map/ppermute | solution.py:52
  168.6 5.8 %collective-permute-start.24 = (f32[1,8,128]{2,1,0:T(8,128)S(1)}, f32[1,8,128]{2,1,0:T(8,128)S(1)}, u32[]{:S(2)}, u32[]{:S(2)}) collective-permute-start(f32[1,8,128]{2,1,0:T(8,128)S(1)} %get-tuple-element.256), channel_id=1, source_target_pairs={{64,0},{128,64},{192,128},{256,192},{320,256},{384,320},{448,384},... | collective-permute-start | bytes 12296 | tf_op jit(solution)/shard_map/ppermute | solution.py:53
  180.1 4.0 %collective-permute-start.26 = (f32[6,1,128]{2,1,0:T(1,128)S(1)}, f32[6,1,128]{2,1,0:T(1,128)S(1)}, u32[]{:S(2)}, u32[]{:S(2)}) collective-permute-start(f32[6,1,128]{2,1,0:T(1,128)S(1)} %get-tuple-element.174), channel_id=1, source_target_pairs={{8,0},{16,8},{24,16},{32,24},{40,32},{48,40},{56,48},{0,56},{9,1},... | collective-permute-start | bytes 9224 | tf_op jit(solution)/shard_map/ppermute | solution.py:53
  184.9 8.2 %collective-permute-start.28 = (f32[6,10,1]{2,1,0:T(8,128)S(1)}, f32[6,10,1]{2,1,0:T(8,128)S(1)}, u32[]{:S(2)}, u32[]{:S(2)}) collective-permute-start(f32[6,10,1]{2,1,0:T(8,128)S(1)} %get-tuple-element.161), channel_id=1, source_target_pairs={{1,0},{2,1},{3,2},{4,3},{5,4},{6,5},{7,6},{0,7},{9,8},{10,9},{11,1... | collective-permute-start | bytes 728 | tf_op jit(solution)/shard_map/ppermute | solution.py:53
  198.6 4.4 %collective-permute-start.30 = (f32[19,1,8,128]{3,2,1,0:T(8,128)S(1)}, f32[19,1,8,128]{3,2,1,0:T(8,128)S(1)}, u32[]{:S(2)}, u32[]{:S(2)}) collective-permute-start(f32[19,1,8,128]{3,2,1,0:T(8,128)S(1)} %get-tuple-element.142), channel_id=1, source_target_pairs={{0,64},{64,128},{128,192},{192,256},{256,320},{320,384},{384,448},... | collective-permute-start | bytes 233480 | tf_op jit(solution)/shard_map/ppermute | solution.py:52
  203.1 6.9 %collective-permute-start.31 = (f32[19,1,8,128]{3,2,1,0:T(8,128)S(1)}, f32[19,1,8,128]{3,2,1,0:T(8,128)S(1)}, u32[]{:S(2)}, u32[]{:S(2)}) collective-permute-start(f32[19,1,8,128]{3,2,1,0:T(8,128)S(1)} %get-tuple-element.143), channel_id=1, source_target_pairs={{64,0},{128,64},{192,128},{256,192},{320,256},{384,320},{448,384},... | collective-permute-start | bytes 233480 | tf_op jit(solution)/shard_map/ppermute | solution.py:53
  215.8 5.1 %collective-permute-start.33 = (f32[19,6,1,128]{3,2,1,0:T(1,128)S(1)}, f32[19,6,1,128]{3,2,1,0:T(1,128)S(1)}, u32[]{:S(2)}, u32[]{:S(2)}) collective-permute-start(f32[19,6,1,128]{3,2,1,0:T(1,128)S(1)} %get-tuple-element.135), channel_id=1, source_target_pairs={{8,0},{16,8},{24,16},{32,24},{40,32},{48,40},{56,48},{0,56},{9,1},... | collective-permute-start | bytes 175112 | tf_op jit(solution)/shard_map/ppermute | solution.py:53
  223.2 6.5 %collective-permute-start.34 = (f32[19,6,10,1]{0,3,2,1:T(1,128)S(1)}, f32[19,6,10,1]{0,3,2,1:T(1,128)S(1)}, u32[]{:S(2)}, u32[]{:S(2)}) collective-permute-start(f32[19,6,10,1]{0,3,2,1:T(1,128)S(1)} %copy.2701), channel_id=1, source_target_pairs={{0,1},{1,2},{2,3},{3,4},{4,5},{5,6},{6,7},{7,0},{8,9},{9,10},{10,1... | collective-permute-start | bytes 13688 | tf_op jit(solution)/shard_map/ppermute | solution.py:52
  238.6 5.9 %collective-permute-start.37 = (f32[1,8,128]{2,1,0:T(8,128)S(1)}, f32[1,8,128]{2,1,0:T(8,128)S(1)}, u32[]{:S(2)}, u32[]{:S(2)}) collective-permute-start(f32[1,8,128]{2,1,0:T(8,128)S(1)} %get-tuple-element.218), channel_id=1, source_target_pairs={{0,64},{64,128},{128,192},{192,256},{256,320},{320,384},{384,448},... | collective-permute-start | bytes 12296 | tf_op jit(solution)/shard_map/ppermute | solution.py:52
  244.4 5.4 %collective-permute-start.36 = (f32[1,8,128]{2,1,0:T(8,128)S(1)}, f32[1,8,128]{2,1,0:T(8,128)S(1)}, u32[]{:S(2)}, u32[]{:S(2)}) collective-permute-start(f32[1,8,128]{2,1,0:T(8,128)S(1)} %get-tuple-element.219), channel_id=1, source_target_pairs={{64,0},{128,64},{192,128},{256,192},{320,256},{384,320},{448,384},... | collective-permute-start | bytes 12296 | tf_op jit(solution)/shard_map/ppermute | solution.py:53
  260.7 8.5 %collective-permute-start.40 = (f32[6,10,1]{2,1,0:T(8,128)S(1)}, f32[6,10,1]{2,1,0:T(8,128)S(1)}, u32[]{:S(2)}, u32[]{:S(2)}) collective-permute-start(f32[6,10,1]{2,1,0:T(8,128)S(1)} %get-tuple-element.159), channel_id=1, source_target_pairs={{1,0},{2,1},{3,2},{4,3},{5,4},{6,5},{7,6},{0,7},{9,8},{10,9},{11,1... | collective-permute-start | bytes 728 | tf_op jit(solution)/shard_map/ppermute | solution.py:53
  274.5 6.4 %collective-permute-start.42 = (f32[19,1,8,128]{3,2,1,0:T(8,128)S(1)}, f32[19,1,8,128]{3,2,1,0:T(8,128)S(1)}, u32[]{:S(2)}, u32[]{:S(2)}) collective-permute-start(f32[19,1,8,128]{3,2,1,0:T(8,128)S(1)} %get-tuple-element.140), channel_id=1, source_target_pairs={{0,64},{64,128},{128,192},{192,256},{256,320},{320,384},{384,448},... | collective-permute-start | bytes 233480 | tf_op jit(solution)/shard_map/ppermute | solution.py:52
  280.9 4.9 %collective-permute-start.43 = (f32[19,1,8,128]{3,2,1,0:T(8,128)S(1)}, f32[19,1,8,128]{3,2,1,0:T(8,128)S(1)}, u32[]{:S(2)}, u32[]{:S(2)}) collective-permute-start(f32[19,1,8,128]{3,2,1,0:T(8,128)S(1)} %get-tuple-element.141), channel_id=1, source_target_pairs={{64,0},{128,64},{192,128},{256,192},{320,256},{384,320},{448,384},... | collective-permute-start | bytes 233480 | tf_op jit(solution)/shard_map/ppermute | solution.py:53
  293.3 6.0 %collective-permute-start.45 = (f32[19,6,1,128]{3,2,1,0:T(1,128)S(1)}, f32[19,6,1,128]{3,2,1,0:T(1,128)S(1)}, u32[]{:S(2)}, u32[]{:S(2)}) collective-permute-start(f32[19,6,1,128]{3,2,1,0:T(1,128)S(1)} %get-tuple-element.133), channel_id=1, source_target_pairs={{8,0},{16,8},{24,16},{32,24},{40,32},{48,40},{56,48},{0,56},{9,1},... | collective-permute-start | bytes 175112 | tf_op jit(solution)/shard_map/ppermute | solution.py:53
  301.6 5.9 %collective-permute-start.46 = (f32[19,6,10,1]{0,3,2,1:T(1,128)S(1)}, f32[19,6,10,1]{0,3,2,1:T(1,128)S(1)}, u32[]{:S(2)}, u32[]{:S(2)}) collective-permute-start(f32[19,6,10,1]{0,3,2,1:T(1,128)S(1)} %copy.2707), channel_id=1, source_target_pairs={{0,1},{1,2},{2,3},{3,4},{4,5},{5,6},{6,7},{7,0},{8,9},{9,10},{10,1... | collective-permute-start | bytes 13688 | tf_op jit(solution)/shard_map/ppermute | solution.py:52
  (333 shorter events, 118.8 us)
Async XLA Ops:
  1.6 13.2 %collective-permute-start.1 = (f32[1,8,128]{2,1,0:T(8,128)S(1)}, f32[1,8,128]{2,1,0:T(8,128)S(1)}, u32[]{:S(2)}, u32[]{:S(2)}) collective-permute-start(f32[1,8,128]{2,1,0:T(8,128)S(1)} %get-tuple-element.329), channel_id=1, source_target_pairs={{0,64},{64,128},{128,192},{192,256},{256,320},{320,384},{384,448},... | collective-permute-start | bytes 12296 | tf_op jit(solution)/shard_map/ppermute | solution.py:52
  10.3 8.3 %collective-permute-start = (f32[1,8,128]{2,1,0:T(8,128)S(1)}, f32[1,8,128]{2,1,0:T(8,128)S(1)}, u32[]{:S(2)}, u32[]{:S(2)}) collective-permute-start(f32[1,8,128]{2,1,0:T(8,128)S(1)} %get-tuple-element.330), channel_id=1, source_target_pairs={{64,0},{128,64},{192,128},{256,192},{320,256},{384,320},{448,384},... | collective-permute-start | bytes 12296 | tf_op jit(solution)/shard_map/ppermute | solution.py:53
  18.6 20.2 %collective-permute-start.3 = (f32[6,1,128]{2,1,0:T(1,128)S(1)}, f32[6,1,128]{2,1,0:T(1,128)S(1)}, u32[]{:S(2)}, u32[]{:S(2)}) collective-permute-start(f32[6,1,128]{2,1,0:T(1,128)S(1)} %get-tuple-element.181), channel_id=1, source_target_pairs={{0,8},{8,16},{16,24},{24,32},{32,40},{40,48},{48,56},{56,0},{1,9},... | collective-permute-start | bytes 9224 | tf_op jit(solution)/shard_map/ppermute | solution.py:52
  23.5 15.3 %collective-permute-start.2 = (f32[6,1,128]{2,1,0:T(1,128)S(1)}, f32[6,1,128]{2,1,0:T(1,128)S(1)}, u32[]{:S(2)}, u32[]{:S(2)}) collective-permute-start(f32[6,1,128]{2,1,0:T(1,128)S(1)} %get-tuple-element.182), channel_id=1, source_target_pairs={{8,0},{16,8},{24,16},{32,24},{40,32},{48,40},{56,48},{0,56},{9,1},... | collective-permute-start | bytes 9224 | tf_op jit(solution)/shard_map/ppermute | solution.py:53
  48.8 11.4 %collective-permute-start.6 = (f32[19,1,8,128]{3,2,1,0:T(8,128)S(1)}, f32[19,1,8,128]{3,2,1,0:T(8,128)S(1)}, u32[]{:S(2)}, u32[]{:S(2)}) collective-permute-start(f32[19,1,8,128]{3,2,1,0:T(8,128)S(1)} %get-tuple-element.146), channel_id=1, source_target_pairs={{0,64},{64,128},{128,192},{192,256},{256,320},{320,384},{384,448},... | collective-permute-start | bytes 233480 | tf_op jit(solution)/shard_map/ppermute | solution.py:52
  52.8 9.7 %collective-permute-start.7 = (f32[19,1,8,128]{3,2,1,0:T(8,128)S(1)}, f32[19,1,8,128]{3,2,1,0:T(8,128)S(1)}, u32[]{:S(2)}, u32[]{:S(2)}) collective-permute-start(f32[19,1,8,128]{3,2,1,0:T(8,128)S(1)} %get-tuple-element.147), channel_id=1, source_target_pairs={{64,0},{128,64},{192,128},{256,192},{320,256},{384,320},{448,384},... | collective-permute-start | bytes 233480 | tf_op jit(solution)/shard_map/ppermute | solution.py:53
  62.6 7.1 %collective-permute-start.8 = (f32[19,6,1,128]{3,2,1,0:T(1,128)S(1)}, f32[19,6,1,128]{3,2,1,0:T(1,128)S(1)}, u32[]{:S(2)}, u32[]{:S(2)}) collective-permute-start(f32[19,6,1,128]{3,2,1,0:T(1,128)S(1)} %get-tuple-element.138), channel_id=1, source_target_pairs={{0,8},{8,16},{16,24},{24,32},{32,40},{40,48},{48,56},{56,0},{1,9},... | collective-permute-start | bytes 175112 | tf_op jit(solution)/shard_map/ppermute | solution.py:52
  72.0 10.3 %collective-permute-start.10 = (f32[19,6,10,1]{0,3,2,1:T(1,128)S(1)}, f32[19,6,10,1]{0,3,2,1:T(1,128)S(1)}, u32[]{:S(2)}, u32[]{:S(2)}) collective-permute-start(f32[19,6,10,1]{0,3,2,1:T(1,128)S(1)} %copy.2651), channel_id=1, source_target_pairs={{0,1},{1,2},{2,3},{3,4},{4,5},{5,6},{6,7},{7,0},{8,9},{9,10},{10,1... | collective-permute-start | bytes 13688 | tf_op jit(solution)/shard_map/ppermute | solution.py:52
  88.8 12.2 %collective-permute-start.13 = (f32[1,8,128]{2,1,0:T(8,128)S(1)}, f32[1,8,128]{2,1,0:T(8,128)S(1)}, u32[]{:S(2)}, u32[]{:S(2)}) collective-permute-start(f32[1,8,128]{2,1,0:T(8,128)S(1)} %get-tuple-element.292), channel_id=1, source_target_pairs={{0,64},{64,128},{128,192},{192,256},{256,320},{320,384},{384,448},... | collective-permute-start | bytes 12296 | tf_op jit(solution)/shard_map/ppermute | solution.py:52
  94.5 8.3 %collective-permute-start.12 = (f32[1,8,128]{2,1,0:T(8,128)S(1)}, f32[1,8,128]{2,1,0:T(8,128)S(1)}, u32[]{:S(2)}, u32[]{:S(2)}) collective-permute-start(f32[1,8,128]{2,1,0:T(8,128)S(1)} %get-tuple-element.293), channel_id=1, source_target_pairs={{64,0},{128,64},{192,128},{256,192},{320,256},{384,320},{448,384},... | collective-permute-start | bytes 12296 | tf_op jit(solution)/shard_map/ppermute | solution.py:53
  102.8 7.2 %collective-permute-start.15 = (f32[6,1,128]{2,1,0:T(1,128)S(1)}, f32[6,1,128]{2,1,0:T(1,128)S(1)}, u32[]{:S(2)}, u32[]{:S(2)}) collective-permute-start(f32[6,1,128]{2,1,0:T(1,128)S(1)} %get-tuple-element.177), channel_id=1, source_target_pairs={{0,8},{8,16},{16,24},{24,32},{32,40},{40,48},{48,56},{56,0},{1,9},... | collective-permute-start | bytes 9224 | tf_op jit(solution)/shard_map/ppermute | solution.py:52
  110.7 8.6 %collective-permute-start.16 = (f32[6,10,1]{2,1,0:T(8,128)S(1)}, f32[6,10,1]{2,1,0:T(8,128)S(1)}, u32[]{:S(2)}, u32[]{:S(2)}) collective-permute-start(f32[6,10,1]{2,1,0:T(8,128)S(1)} %get-tuple-element.163), channel_id=1, source_target_pairs={{1,0},{2,1},{3,2},{4,3},{5,4},{6,5},{7,6},{0,7},{9,8},{10,9},{11,1... | collective-permute-start | bytes 728 | tf_op jit(solution)/shard_map/ppermute | solution.py:53
  123.7 11.3 %collective-permute-start.18 = (f32[19,1,8,128]{3,2,1,0:T(8,128)S(1)}, f32[19,1,8,128]{3,2,1,0:T(8,128)S(1)}, u32[]{:S(2)}, u32[]{:S(2)}) collective-permute-start(f32[19,1,8,128]{3,2,1,0:T(8,128)S(1)} %get-tuple-element.144), channel_id=1, source_target_pairs={{0,64},{64,128},{128,192},{192,256},{256,320},{320,384},{384,448},... | collective-permute-start | bytes 233480 | tf_op jit(solution)/shard_map/ppermute | solution.py:52
  128.2 9.0 %collective-permute-start.19 = (f32[19,1,8,128]{3,2,1,0:T(8,128)S(1)}, f32[19,1,8,128]{3,2,1,0:T(8,128)S(1)}, u32[]{:S(2)}, u32[]{:S(2)}) collective-permute-start(f32[19,1,8,128]{3,2,1,0:T(8,128)S(1)} %get-tuple-element.145), channel_id=1, source_target_pairs={{64,0},{128,64},{192,128},{256,192},{320,256},{384,320},{448,384},... | collective-permute-start | bytes 233480 | tf_op jit(solution)/shard_map/ppermute | solution.py:53
  146.4 11.5 %collective-permute-start.22 = (f32[19,6,10,1]{0,3,2,1:T(1,128)S(1)}, f32[19,6,10,1]{0,3,2,1:T(1,128)S(1)}, u32[]{:S(2)}, u32[]{:S(2)}) collective-permute-start(f32[19,6,10,1]{0,3,2,1:T(1,128)S(1)} %copy.2695), channel_id=1, source_target_pairs={{0,1},{1,2},{2,3},{3,4},{4,5},{5,6},{6,7},{7,0},{8,9},{9,10},{10,1... | collective-permute-start | bytes 13688 | tf_op jit(solution)/shard_map/ppermute | solution.py:52
  163.1 12.3 %collective-permute-start.25 = (f32[1,8,128]{2,1,0:T(8,128)S(1)}, f32[1,8,128]{2,1,0:T(8,128)S(1)}, u32[]{:S(2)}, u32[]{:S(2)}) collective-permute-start(f32[1,8,128]{2,1,0:T(8,128)S(1)} %get-tuple-element.255), channel_id=1, source_target_pairs={{0,64},{64,128},{128,192},{192,256},{256,320},{320,384},{384,448},... | collective-permute-start | bytes 12296 | tf_op jit(solution)/shard_map/ppermute | solution.py:52
  168.6 8.4 %collective-permute-start.24 = (f32[1,8,128]{2,1,0:T(8,128)S(1)}, f32[1,8,128]{2,1,0:T(8,128)S(1)}, u32[]{:S(2)}, u32[]{:S(2)}) collective-permute-start(f32[1,8,128]{2,1,0:T(8,128)S(1)} %get-tuple-element.256), channel_id=1, source_target_pairs={{64,0},{128,64},{192,128},{256,192},{320,256},{384,320},{448,384},... | collective-permute-start | bytes 12296 | tf_op jit(solution)/shard_map/ppermute | solution.py:53
  177.0 7.7 %collective-permute-start.27 = (f32[6,1,128]{2,1,0:T(1,128)S(1)}, f32[6,1,128]{2,1,0:T(1,128)S(1)}, u32[]{:S(2)}, u32[]{:S(2)}) collective-permute-start(f32[6,1,128]{2,1,0:T(1,128)S(1)} %get-tuple-element.173), channel_id=1, source_target_pairs={{0,8},{8,16},{16,24},{24,32},{32,40},{40,48},{48,56},{56,0},{1,9},... | collective-permute-start | bytes 9224 | tf_op jit(solution)/shard_map/ppermute | solution.py:52
  184.9 10.2 %collective-permute-start.28 = (f32[6,10,1]{2,1,0:T(8,128)S(1)}, f32[6,10,1]{2,1,0:T(8,128)S(1)}, u32[]{:S(2)}, u32[]{:S(2)}) collective-permute-start(f32[6,10,1]{2,1,0:T(8,128)S(1)} %get-tuple-element.161), channel_id=1, source_target_pairs={{1,0},{2,1},{3,2},{4,3},{5,4},{6,5},{7,6},{0,7},{9,8},{10,9},{11,1... | collective-permute-start | bytes 728 | tf_op jit(solution)/shard_map/ppermute | solution.py:53
  198.6 11.3 %collective-permute-start.30 = (f32[19,1,8,128]{3,2,1,0:T(8,128)S(1)}, f32[19,1,8,128]{3,2,1,0:T(8,128)S(1)}, u32[]{:S(2)}, u32[]{:S(2)}) collective-permute-start(f32[19,1,8,128]{3,2,1,0:T(8,128)S(1)} %get-tuple-element.142), channel_id=1, source_target_pairs={{0,64},{64,128},{128,192},{192,256},{256,320},{320,384},{384,448},... | collective-permute-start | bytes 233480 | tf_op jit(solution)/shard_map/ppermute | solution.py:52
  203.1 10.7 %collective-permute-start.31 = (f32[19,1,8,128]{3,2,1,0:T(8,128)S(1)}, f32[19,1,8,128]{3,2,1,0:T(8,128)S(1)}, u32[]{:S(2)}, u32[]{:S(2)}) collective-permute-start(f32[19,1,8,128]{3,2,1,0:T(8,128)S(1)} %get-tuple-element.143), channel_id=1, source_target_pairs={{64,0},{128,64},{192,128},{256,192},{320,256},{384,320},{448,384},... | collective-permute-start | bytes 233480 | tf_op jit(solution)/shard_map/ppermute | solution.py:53
  213.8 7.1 %collective-permute-start.32 = (f32[19,6,1,128]{3,2,1,0:T(1,128)S(1)}, f32[19,6,1,128]{3,2,1,0:T(1,128)S(1)}, u32[]{:S(2)}, u32[]{:S(2)}) collective-permute-start(f32[19,6,1,128]{3,2,1,0:T(1,128)S(1)} %get-tuple-element.134), channel_id=1, source_target_pairs={{0,8},{8,16},{16,24},{24,32},{32,40},{40,48},{48,56},{56,0},{1,9},... | collective-permute-start | bytes 175112 | tf_op jit(solution)/shard_map/ppermute | solution.py:52
  223.2 9.9 %collective-permute-start.34 = (f32[19,6,10,1]{0,3,2,1:T(1,128)S(1)}, f32[19,6,10,1]{0,3,2,1:T(1,128)S(1)}, u32[]{:S(2)}, u32[]{:S(2)}) collective-permute-start(f32[19,6,10,1]{0,3,2,1:T(1,128)S(1)} %copy.2701), channel_id=1, source_target_pairs={{0,1},{1,2},{2,3},{3,4},{4,5},{5,6},{6,7},{7,0},{8,9},{9,10},{10,1... | collective-permute-start | bytes 13688 | tf_op jit(solution)/shard_map/ppermute | solution.py:52
  238.6 12.3 %collective-permute-start.37 = (f32[1,8,128]{2,1,0:T(8,128)S(1)}, f32[1,8,128]{2,1,0:T(8,128)S(1)}, u32[]{:S(2)}, u32[]{:S(2)}) collective-permute-start(f32[1,8,128]{2,1,0:T(8,128)S(1)} %get-tuple-element.218), channel_id=1, source_target_pairs={{0,64},{64,128},{128,192},{192,256},{256,320},{320,384},{384,448},... | collective-permute-start | bytes 12296 | tf_op jit(solution)/shard_map/ppermute | solution.py:52
  244.4 8.3 %collective-permute-start.36 = (f32[1,8,128]{2,1,0:T(8,128)S(1)}, f32[1,8,128]{2,1,0:T(8,128)S(1)}, u32[]{:S(2)}, u32[]{:S(2)}) collective-permute-start(f32[1,8,128]{2,1,0:T(8,128)S(1)} %get-tuple-element.219), channel_id=1, source_target_pairs={{64,0},{128,64},{192,128},{256,192},{320,256},{384,320},{448,384},... | collective-permute-start | bytes 12296 | tf_op jit(solution)/shard_map/ppermute | solution.py:53
  252.7 7.1 %collective-permute-start.39 = (f32[6,1,128]{2,1,0:T(1,128)S(1)}, f32[6,1,128]{2,1,0:T(1,128)S(1)}, u32[]{:S(2)}, u32[]{:S(2)}) collective-permute-start(f32[6,1,128]{2,1,0:T(1,128)S(1)} %get-tuple-element.169), channel_id=1, source_target_pairs={{0,8},{8,16},{16,24},{24,32},{32,40},{40,48},{48,56},{56,0},{1,9},... | collective-permute-start | bytes 9224 | tf_op jit(solution)/shard_map/ppermute | solution.py:52
  260.7 10.7 %collective-permute-start.40 = (f32[6,10,1]{2,1,0:T(8,128)S(1)}, f32[6,10,1]{2,1,0:T(8,128)S(1)}, u32[]{:S(2)}, u32[]{:S(2)}) collective-permute-start(f32[6,10,1]{2,1,0:T(8,128)S(1)} %get-tuple-element.159), channel_id=1, source_target_pairs={{1,0},{2,1},{3,2},{4,3},{5,4},{6,5},{7,6},{0,7},{9,8},{10,9},{11,1... | collective-permute-start | bytes 728 | tf_op jit(solution)/shard_map/ppermute | solution.py:53
  274.5 12.0 %collective-permute-start.42 = (f32[19,1,8,128]{3,2,1,0:T(8,128)S(1)}, f32[19,1,8,128]{3,2,1,0:T(8,128)S(1)}, u32[]{:S(2)}, u32[]{:S(2)}) collective-permute-start(f32[19,1,8,128]{3,2,1,0:T(8,128)S(1)} %get-tuple-element.140), channel_id=1, source_target_pairs={{0,64},{64,128},{128,192},{192,256},{256,320},{320,384},{384,448},... | collective-permute-start | bytes 233480 | tf_op jit(solution)/shard_map/ppermute | solution.py:52
  280.9 9.4 %collective-permute-start.43 = (f32[19,1,8,128]{3,2,1,0:T(8,128)S(1)}, f32[19,1,8,128]{3,2,1,0:T(8,128)S(1)}, u32[]{:S(2)}, u32[]{:S(2)}) collective-permute-start(f32[19,1,8,128]{3,2,1,0:T(8,128)S(1)} %get-tuple-element.141), channel_id=1, source_target_pairs={{64,0},{128,64},{192,128},{256,192},{320,256},{384,320},{448,384},... | collective-permute-start | bytes 233480 | tf_op jit(solution)/shard_map/ppermute | solution.py:53
  290.3 9.0 %collective-permute-start.44 = (f32[19,6,1,128]{3,2,1,0:T(1,128)S(1)}, f32[19,6,1,128]{3,2,1,0:T(1,128)S(1)}, u32[]{:S(2)}, u32[]{:S(2)}) collective-permute-start(f32[19,6,1,128]{3,2,1,0:T(1,128)S(1)} %get-tuple-element.132), channel_id=1, source_target_pairs={{0,8},{8,16},{16,24},{24,32},{32,40},{40,48},{48,56},{56,0},{1,9},... | collective-permute-start | bytes 175112 | tf_op jit(solution)/shard_map/ppermute | solution.py:52
  293.3 7.2 %collective-permute-start.45 = (f32[19,6,1,128]{3,2,1,0:T(1,128)S(1)}, f32[19,6,1,128]{3,2,1,0:T(1,128)S(1)}, u32[]{:S(2)}, u32[]{:S(2)}) collective-permute-start(f32[19,6,1,128]{3,2,1,0:T(1,128)S(1)} %get-tuple-element.133), channel_id=1, source_target_pairs={{8,0},{16,8},{24,16},{32,24},{40,32},{48,40},{56,48},{0,56},{9,1},... | collective-permute-start | bytes 175112 | tf_op jit(solution)/shard_map/ppermute | solution.py:53
  301.6 9.8 %collective-permute-start.46 = (f32[19,6,10,1]{0,3,2,1:T(1,128)S(1)}, f32[19,6,10,1]{0,3,2,1:T(1,128)S(1)}, u32[]{:S(2)}, u32[]{:S(2)}) collective-permute-start(f32[19,6,10,1]{0,3,2,1:T(1,128)S(1)} %copy.2707), channel_id=1, source_target_pairs={{0,1},{1,2},{2,3},{3,4},{4,5},{5,6},{6,7},{7,0},{8,9},{9,10},{10,1... | collective-permute-start | bytes 13688 | tf_op jit(solution)/shard_map/ppermute | solution.py:52
  (17 other events, 83.6 us)
where the time goes:
time: 323 us; the launch traced here: 318 us
  starting transfers between devices  237 us (73%)
  waiting for transfers between devices  40 us (12%)
  local copies, waits for them, and re-layouts  21 us (7%)
  other arithmetic  15.5 us (5%)
    ppermute x24, starting transfers between devices, extended(): after = lax.ppermute(first, axis, down)  133 us
    ppermute x24, starting transfers between devices, extended(): before = lax.ppermute(last, axis, up)  104 us
    ppermute x24, waiting for transfers between devices, extended(): after = lax.ppermute(first, axis, down)  33.3 us
    ppermute x24, waiting for transfers between devices, extended(): before = lax.ppermute(last, axis, up)  6.65 us
  transfers between devices with their start and end apart: 48, of which 25 were waited for; matrix products, arithmetic and copies ran while one was open for 4% of the time, Pallas kernels for 0%

commit v1 on v0

v1 whole, which is shorter than its diff:
```python
import functools
import math

import jax
import jax.numpy as jnp
from jax import lax
from jax.experimental import pallas as pl
from jax.experimental.pallas import tpu as pltpu
from jax.sharding import PartitionSpec as P

STEPS = 4
MESH = pl.DeviceIdType.MESH
velocities = [
    (0, 0, 0),
    (1, 0, 0), (-1, 0, 0), (0, 1, 0), (0, -1, 0), (0, 0, 1), (0, 0, -1),
    (1, 1, 0), (-1, -1, 0), (1, -1, 0), (-1, 1, 0),
    (1, 0, 1), (-1, 0, -1), (1, 0, -1), (-1, 0, 1),
    (0, 1, 1), (0, -1, -1), (0, 1, -1), (0, -1, 1),
]
opposite = [0, 2, 1, 4, 3, 6, 5, 8, 7, 10, 9, 12, 11, 14, 13, 16, 15, 18, 17]
ROWS = 4
IN_ROWS = 24
OUT_ROWS = 16

offsets = [(1, 0), (-1, 0), (0, 1), (0, -1), (1, 1), (1, -1), (-1, 1), (-1, -1)]


def in_block(x, y, e):
    return x == e[0] and ROWS * e[1] <= y < ROWS * e[1] + ROWS


pops_of = {
    e: [
        (i, c)
        for c in range(ROWS)
        for i in range(19)
        if in_block(velocities[i][0], c + velocities[i][1], e)
    ]
    for e in offsets
}
start_of, total = {}, 0
for e in offsets:
    start_of[e] = total
    total += len(pops_of[e])
TOTAL = total


def pseudo_potential(rho):
    gap = 1.0 - rho
    square = rho * rho
    pressure = rho * 0.06 * (1.0 + rho + square - square * rho) / (gap * gap * gap) - square
    return jnp.sqrt(6.0 * (rho * (1.0 / 3.0) - pressure))


def equilibrium(rho, u):
    ux, uy, uz = u
    base = 1.0 - 1.5 * (ux * ux + uy * uy + uz * uz)
    third, axis, diagonal = rho * (1.0 / 3.0), rho * (1.0 / 18.0), rho * (1.0 / 36.0)
    out = [third * base]

    def pair(weight, projection):
        even = base + 4.5 * projection * projection
        odd = 3.0 * projection
        out.append(weight * (even + odd))
        out.append(weight * (even - odd))

    for value in (ux, uy, uz):
        pair(axis, value)
    for a, b in ((ux, uy), (ux, uz), (uy, uz)):
        pair(diagonal, a + b)
        pair(diagonal, a - b)
    return out


def density_and_momentum(f):
    s = {k: f[k] + f[k + 1] for k in range(1, 19, 2)}
    d = {k: f[k] - f[k + 1] for k in range(1, 19, 2)}
    rho = f[0] + (s[1] + s[3] + s[5]) + ((s[7] + s[9]) + (s[11] + s[13]) + (s[15] + s[17]))
    jx = d[1] + (d[7] + d[9]) + (d[11] + d[13])
    jy = d[3] + (d[7] - d[9]) + (d[15] + d[17])
    jz = d[5] + (d[11] - d[13]) + (d[15] - d[17])
    return rho, (jx, jy, jz)


def collide(f, force_over, solid):
    s = {k: f[k] + f[k + 1] for k in range(1, 19, 2)}
    d = {k: f[k] - f[k + 1] for k in range(1, 19, 2)}
    sx, sy, sz = s[1], s[3], s[5]
    sxy, sxz, syz = s[7] + s[9], s[11] + s[13], s[15] + s[17]
    pxy, pxz, pyz = s[7] - s[9], s[11] - s[13], s[15] - s[17]
    xy_x, xy_y = d[7] + d[9], d[7] - d[9]
    xz_x, xz_z = d[11] + d[13], d[11] - d[13]
    yz_y, yz_z = d[15] + d[17], d[15] - d[17]
    axes, diagonals = sx + sy + sz, sxy + sxz + syz
    rho = f[0] + axes + diagonals
    tx, ty, tz = xy_x + xz_x, xy_y + yz_y, xz_z + yz_z
    jx, jy, jz = d[1] + tx, d[3] + ty, d[5] + tz
    inverse = 1.0 / rho
    fx, fy, fz = force_over
    ux, uy, uz = jx * inverse, jy * inverse, jz * inverse
    vx, vy, vz = ux + fx * inverse, uy + fy * inverse, uz + fz * inverse
    exx, eyy, ezz = jx * ux, jy * uy, jz * uz
    exy, exz, eyz = jx * uy, jx * uz, jy * uz
    wx, wy, wz = rho * vx, rho * vy, rho * vz
    dxx, dyy, dzz = wx * vx - exx, wy * vy - eyy, wz * vz - ezz
    dxy, dxz, dyz = wx * vy - exy, wx * vz - exz, wy * vz - eyz
    e2, d2 = exx + eyy + ezz, dxx + dyy + dzz
    g_e = (1.19 * (-11.0 * rho + 19.0 * e2 - (-30.0 * f[0] - 11.0 * axes + 8.0 * diagonals)) + 19.0 * d2) * (1.0 / 2394.0)
    g_eps = (1.4 * (3.0 * rho - 5.5 * e2 - (12.0 * f[0] - 4.0 * axes + diagonals)) - 5.5 * d2) * (1.0 / 252.0)
    pxx_a, pxx_d = 3.0 * sx - axes, diagonals - 3.0 * syz
    pww_a, pww_d = sy - sz, sxy - sxz
    exx_e, dxx_e = 3.0 * exx - e2, 3.0 * dxx - d2
    eww_e, dww_e = eyy - ezz, dyy - dzz
    g_pxx = (1.25 * (exx_e - (pxx_a + pxx_d)) + dxx_e) * (1.0 / 36.0)
    g_pixx = (1.4 * (2.0 * pxx_a - pxx_d - 0.5 * exx_e) - 0.5 * dxx_e) * (1.0 / 72.0)
    g_pww = (1.25 * (eww_e - (pww_a + pww_d)) + dww_e) * (1.0 / 12.0)
    g_piww = (1.4 * (2.0 * pww_a - pww_d - 0.5 * eww_e) - 0.5 * dww_e) * (1.0 / 24.0)
    g_pxy = (1.25 * (exy - pxy) + dxy) * 0.25
    g_pxz = (1.25 * (exz - pxz) + dxz) * 0.25
    g_pyz = (1.25 * (eyz - pyz) + dyz) * 0.25

    def odd(j, axis, t, push):
        g_q = (1.2 * ((-2.0 / 3.0) * j + 4.0 * axis - t) - (2.0 / 3.0) * push) * (1.0 / 40.0)
        g_j = push * 0.1
        return g_j - 4.0 * g_q, g_j + g_q

    ax, bx = odd(jx, d[1], tx, fx)
    ay, by = odd(jy, d[3], ty, fy)
    az, bz = odd(jz, d[5], tz, fz)
    m = -1.98 / 8.0
    mx, my, mz = m * (xy_x - xz_x), m * (yz_y - xy_y), m * (xz_z - yz_z)
    axis_all = -11.0 * g_e - 4.0 * g_eps
    diagonal_all = 8.0 * g_e + g_eps
    part_x = g_pxx - 2.0 * g_pixx
    part_w = g_pww - 2.0 * g_piww
    even_x = axis_all + 2.0 * part_x
    even_y = axis_all - part_x + part_w
    even_z = axis_all - part_x - part_w
    both_x, both_w = g_pxx + g_pixx, g_pww + g_piww
    even_xy = diagonal_all + both_x + both_w
    even_xz = diagonal_all + both_x - both_w
    even_yz = diagonal_all - 2.0 * both_x
    cxy, cyx = bx + mx, by - my
    cxz, czx = bx - mx, bz + mz
    cyz, czy = by + my, bz - mz
    change = [12.0 * g_eps - 30.0 * g_e]

    def pair(even, odd_part):
        change.append(even + odd_part)
        change.append(even - odd_part)

    pair(even_x, ax)
    pair(even_y, ay)
    pair(even_z, az)
    pair(even_xy + g_pxy, cxy + cyx)
    pair(even_xy - g_pxy, cxy - cyx)
    pair(even_xz + g_pxz, cxz + czx)
    pair(even_xz - g_pxz, cxz - czx)
    pair(even_yz + g_pyz, cyz + czy)
    pair(even_yz - g_pyz, cyz - czy)
    return [jnp.where(solid, f[opposite[i]], f[i] + change[i]) for i in range(19)]


def kernel(
    sizes,
    scatter_hbm, speed_hbm, bubble_hbm, wall_hbm,
    density_out, velocity_out,
    scatter, speed, bubble, wall,
    in_send, in_recv, out_send, out_recv,
    psi, psi_x, psi_rest,
    pops, solids,
    send, recv,
    load_sem, in_sems, out_sems, psi_sems, round_sems,
):
    nx, ny, nz = sizes
    gx, gy, gz = lax.axis_index("gx"), lax.axis_index("gy"), lax.axis_index("gz")
    planes, groups = nx * 4, ny * 2
    X = gx * 4 + lax.div(gz, 2)
    Y = gy * 2 + lax.rem(gz, 2)

    def neighbour(e):
        x, y = lax.rem(X + (e[0] + planes), planes), lax.rem(Y + (e[1] + groups), groups)
        return {
            "gx": lax.div(x, 4),
            "gy": lax.div(y, 2),
            "gz": lax.rem(x, 4) * 2 + lax.rem(y, 2),
        }

    loads = [
        pltpu.make_async_copy(src, dst, load_sem.at[k])
        for k, (src, dst) in enumerate(
            ((scatter_hbm, scatter), (speed_hbm, speed), (bubble_hbm, bubble), (wall_hbm, wall))
        )
    ]
    for load in loads:
        load.start()
    barrier = pltpu.get_barrier_semaphore()
    where_to = [neighbour(e) for e in offsets]
    peers = [lax.rem(gz + k, nz) for k in range(1, nz)]
    for target in where_to + [{"gx": gx, "gy": gy, "gz": peer} for peer in peers]:
        pl.semaphore_signal(barrier, inc=1, device_id=target, device_id_type=MESH)
    for load in loads:
        load.wait()

    for p in range(4):
        rho0 = jnp.where(bubble[p] == 1, 0.06, 0.28) * scatter[p]
        solid = jnp.where(wall[p] == 1, 1.0, 0.0)
        fields = [rho0, speed[0, p], speed[1, p], speed[2, p], solid]
        for half in range(2):
            first = (p * 2 + half) * IN_ROWS
            for k, field in enumerate(fields):
                in_send[first + k * ROWS : first + (k + 1) * ROWS, :] = field[half * ROWS : (half + 1) * ROWS]
    pl.semaphore_wait(barrier, len(where_to) + len(peers))

    def exchange(source, target, rows, sems):
        mine = pl.ds(pl.multiple_of(gz * rows, 8), rows)
        copies = []
        for k, peer in enumerate(peers):
            copy = pltpu.make_async_remote_copy(
                src_ref=source.at[pl.ds(pl.multiple_of(peer * rows, 8), rows), :],
                dst_ref=target.at[mine, :],
                send_sem=sems.at[0, k],
                recv_sem=sems.at[1, k],
                device_id={"gx": gx, "gy": gy, "gz": peer},
                device_id_type=MESH,
            )
            copy.start()
            copies.append(copy)
        target[mine, :] = source[mine, :]
        for copy in copies:
            copy.wait()

    exchange(in_send, in_recv, IN_ROWS, in_sems)

    def line(field, c):
        return in_recv[pl.ds(field * ROWS + c, 8, stride=IN_ROWS), :]

    for c in range(ROWS):
        solids[c] = line(4, c)
        for i, value in enumerate(equilibrium(line(0, c), (line(1, c), line(2, c), line(3, c)))):
            pops[0, i, c] = value

    lane = lax.broadcasted_iota(jnp.int32, (8, 128), 1)
    is_first, is_last = lane == 0, lane == 127

    def shift(v, by):
        rolled = pltpu.roll(v, 1 if by > 0 else 127, 1)
        carried = pltpu.roll(rolled, 1 if by > 0 else 7, 0)
        return jnp.where(is_first if by > 0 else is_last, carried, rolled)

    def step(r, now, later):
        for c in range(ROWS):
            rho, _ = density_and_momentum([pops[now, i, c] for i in range(19)])
            psi[r, c] = jnp.where(solids[c] > 0.5, 0.5, pseudo_potential(rho))
        copies = []
        for k, e in enumerate(offsets):
            if e[1] == 0:
                source, target = psi.at[r], psi_x.at[r, k]
            else:
                source, target = psi.at[r, ROWS - 1 if e[1] > 0 else 0], psi_rest.at[r, k - 2]
            copies.append(
                pltpu.make_async_remote_copy(
                    src_ref=source,
                    dst_ref=target,
                    send_sem=psi_sems.at[0, r, k],
                    recv_sem=psi_sems.at[1, r, k],
                    device_id=where_to[k],
                    device_id_type=MESH,
                )
            )
            copies[-1].start()
        for copy in copies:
            copy.wait()

        def at(x, y):
            side = -1 if y < 0 else (1 if y >= ROWS else 0)
            if (x, side) == (0, 0):
                return psi[r, y]
            k = offsets.index((-x, -side))
            return psi_x[r, k, y] if side == 0 else psi_rest[r, k - 2]

        for c in range(ROWS):
            here = at(0, c)
            spread = [at(1, y) - at(-1, y) for y in (c - 1, c, c + 1)]
            left, middle, right = [at(x, c + 1) - at(x, c - 1) for x in (-1, 0, 1)]
            around = 2.0 * here + ((at(-1, c) + at(1, c)) + (at(0, c - 1) + at(0, c + 1)))
            scale = here * (1.0 / 36.0)
            force = (
                scale * ((2.0 * spread[1] + (spread[0] + spread[2])) + (shift(spread[1], 1) + shift(spread[1], -1))),
                scale * ((2.0 * middle + (left + right)) + (shift(middle, 1) + shift(middle, -1))),
                scale * (shift(around, -1) - shift(around, 1)),
            )
            post = collide([pops[now, i, c] for i in range(19)], force, solids[c] > 0.5)
            for i, (cx, cy, cz) in enumerate(velocities):
                value = shift(post[i], cz) if cz else post[i]
                if in_block(cx, c + cy, (0, 0)):
                    pops[later, i, c + cy] = value
                else:
                    for e in offsets:
                        if in_block(cx, c + cy, e):
                            send[r, start_of[e] + pops_of[e].index((i, c))] = value
        copies = []
        for k, e in enumerate(offsets):
            part = pl.ds(start_of[e], len(pops_of[e]))
            copies.append(
                pltpu.make_async_remote_copy(
                    src_ref=send.at[r, part],
                    dst_ref=recv.at[r, part],
                    send_sem=round_sems.at[0, r, k],
                    recv_sem=round_sems.at[1, r, k],
                    device_id=where_to[k],
                    device_id_type=MESH,
                )
            )
            copies[-1].start()
        for copy in copies:
            copy.wait()
        for e in offsets:
            for k, (i, c) in enumerate(pops_of[e]):
                pops[later, i, c + velocities[i][1] - ROWS * e[1]] = recv[r, start_of[e] + k]

    def body(r, carry):
        now = lax.rem(r, 2)
        step(r, now, 1 - now)
        return carry

    lax.fori_loop(0, STEPS, body, 0)

    for c in range(ROWS):
        rho, momentum = density_and_momentum([pops[STEPS % 2, i, c] for i in range(19)])
        fluid = solids[c] < 0.5
        scale = math.sqrt(3.0) / rho
        fields = [rho * (1.0 / 0.28)] + [j * scale for j in momentum]
        for k, field in enumerate(fields):
            out_send[pl.ds(k * ROWS + c, 8, stride=OUT_ROWS), :] = jnp.where(fluid, field, 0.0)
    exchange(out_send, out_recv, OUT_ROWS, out_sems)
    for p in range(4):
        for half in range(2):
            first = (p * 2 + half) * OUT_ROWS
            rows = slice(half * ROWS, (half + 1) * ROWS)
            density_out[p, rows, :] = out_recv[first : first + ROWS, :]
            for k in range(3):
                velocity_out[k, p, rows, :] = out_recv[first + (k + 1) * ROWS : first + (k + 2) * ROWS, :]


def solution(mesh):
    sizes = (mesh.shape["gx"], mesh.shape["gy"], mesh.shape["gz"])
    block = (4, 8, 128)
    tile = (8, 128)

    def on_device(density_scatter, initial_velocity, bubble_mask, wall_flags):
        return tuple(
            pl.pallas_call(
                functools.partial(kernel, sizes),
                out_shape=[
                    jax.ShapeDtypeStruct(block, jnp.float32),
                    jax.ShapeDtypeStruct((3,) + block, jnp.float32),
                ],
                in_specs=[pl.BlockSpec(memory_space=pl.ANY)] * 4,
                out_specs=[pl.BlockSpec(memory_space=pltpu.VMEM)] * 2,
                scratch_shapes=[
                    pltpu.VMEM(block, jnp.float32),
                    pltpu.VMEM((3,) + block, jnp.float32),
                    pltpu.VMEM(block, jnp.int32),
                    pltpu.VMEM(block, jnp.int32),
                    pltpu.VMEM((8 * IN_ROWS, 128), jnp.float32),
                    pltpu.VMEM((8 * IN_ROWS, 128), jnp.float32),
                    pltpu.VMEM((8 * OUT_ROWS, 128), jnp.float32),
                    pltpu.VMEM((8 * OUT_ROWS, 128), jnp.float32),
                    pltpu.VMEM((STEPS, ROWS) + tile, jnp.float32),
                    pltpu.VMEM((STEPS, 2, ROWS) + tile, jnp.float32),
                    pltpu.VMEM((STEPS, 6) + tile, jnp.float32),
                    pltpu.VMEM((2, 19, ROWS) + tile, jnp.float32),
                    pltpu.VMEM((ROWS,) + tile, jnp.float32),
                    pltpu.VMEM((STEPS, TOTAL) + tile, jnp.float32),
                    pltpu.VMEM((STEPS, TOTAL) + tile, jnp.float32),
                    pltpu.SemaphoreType.DMA((4,)),
                    pltpu.SemaphoreType.DMA((2, 7)),
                    pltpu.SemaphoreType.DMA((2, 7)),
                    pltpu.SemaphoreType.DMA((2, STEPS, 8)),
                    pltpu.SemaphoreType.DMA((2, STEPS, 8)),
                ],
                compiler_params=pltpu.CompilerParams(collective_id=0, has_side_effects=True),
            )(density_scatter, initial_velocity, bubble_mask, wall_flags)
        )

    return jax.shard_map(
        on_device,
        mesh=mesh,
        in_specs=(
            P("gx", "gy", "gz"),
            P(None, "gx", "gy", "gz"),
            P("gx", "gy", "gz"),
            P("gx", "gy", "gz"),
        ),
        out_specs=(P("gx", "gy", "gz"), P(None, "gx", "gy", "gz")),
        check_vma=False,
    )
```

time: 323 us -> 78.8 us (0.24); the launches traced: 318 us -> 78.4 us
  starting transfers between devices: 237 us -> 0 us
  Pallas kernels: 0 us -> 75 us
  waiting for transfers between devices: 40 us -> 0 us
  local copies, waits for them, and re-layouts: 21 us -> 2.74 us
  other arithmetic: 15.5 us -> 0 us
    ppermute x48 -> x0, starting transfers between devices: 237 us -> none  [the longest x24 133 us: extended(): after = lax.ppermute(first, axis, down)]
    pallas_call x0 -> x1, Pallas kernels: none -> 75 us  [on_device(): pl.pallas_call(functools.partial(kernel, sizes), out_shape=[jax.ShapeDtyp...]
    ppermute x48 -> x0, waiting for transfers between devices: 40 us -> none  [the longest x24 33.3 us: extended(): after = lax.ppermute(first, axis, down)]
    ppermute x8 -> x0, local copies, waits for them, and re-layouts: 8.42 us -> none  [the longest x4 4.21 us: extended(): before = lax.ppermute(last, axis, up)]
    concatenate x20 -> x0, other arithmetic: 6.06 us -> none  [extended(): shard = jnp.concatenate([before, shard, after], axis=dim)]
    slice x24 -> x0, local copies, waits for them, and re-layouts: 5.99 us -> none  [the longest x16 3.53 us: extended(): last = lax.slice_in_dim(shard, length - width, length, axis=dim)]
    select_n x10 -> x0, other arithmetic: 3.49 us -> none  [the longest x4 1.4 us: on_device(): jnp.where(solid, wall_potential, pseudo_potential(mass_per_volume))]
  transfers between devices with their start and end apart: 48 -> 0, of which waited for: 25 -> 0; matrix products, arithmetic and copies ran while one was open for 4% -> 0% of each run, Pallas kernels for 0% -> 0%
where the time goes in v1:
time: 78.8 us; the launch traced here: 78.4 us
  Pallas kernels  75 us (95%)
  local copies, waits for them, and re-layouts  2.74 us (3%)
    pallas_call x1, Pallas kernels, on_device(): pl.pallas_call(functools.partial(kernel, sizes), out_shape=[jax.ShapeDtyp...  75 us
    unnamed x2, local copies, waits for them, and re-layouts  2.74 us

profile of v1, /device:TPU:1, one launch (start us, length us, event | category | flops | bytes accessed | tf_op | source)
XLA Modules:
  0.0 78.4 jit_solution(1885532941044700269)
XLA Ops:
  0.6 75.0 %shard_map.59 = (f32[4,8,128]{2,1,0:T(8,128)}, f32[3,4,8,128]{3,2,1,0:T(8,128)}) custom-call(f32[4,8,128]{2,1,0:T(8,128)} %scatter_hbm.1, f32[3,4,8,128]{3,2,1,0:T(8,128)} %speed_hbm.1, s32[4,8,128]{2,1,0:T(8,128)} %bubble_hbm.1, s32[4,8,128]{2,1,0:T(8,128)} %wall_hbm.1), custom_call_target="tpu_custom_call" | custom-call | tf_op jit(solution)/shard_map/pallas_call | solution.py:353
  75.7 1.3 %copy.8 = f32[4,8,128]{2,1,0:T(8,128)} copy(f32[4,8,128]{2,1,0:T(8,128)} %get-tuple-element.4) | data formatting | bytes 32768
  77.0 1.4 %copy.9 = f32[3,4,8,128]{3,2,1,0:T(8,128)} copy(f32[3,4,8,128]{3,2,1,0:T(8,128)} %get-tuple-element.5) | data formatting | bytes 98304

commit v2 on v1

--- a/solution.py
+++ b/solution.py
@@ -23,10 +23,16 @@
 OUT_ROWS = 16
 
 offsets = [(1, 0), (-1, 0), (0, 1), (0, -1), (1, 1), (1, -1), (-1, 1), (-1, -1)]
+far = [(2, 1), (2, -1), (-2, 1), (-2, -1), (2, 0), (-2, 0)]
 
 
 def in_block(x, y, e):
     return x == e[0] and ROWS * e[1] <= y < ROWS * e[1] + ROWS
+
+
+def in_halo(x, y, e):
+    near = abs(x - e[0]) <= 1 and ROWS * e[1] - 1 <= y <= ROWS * e[1] + ROWS
+    return near and not in_block(x, y, e)
 
 
 pops_of = {
@@ -36,12 +42,16 @@
         for i in range(19)
         if in_block(velocities[i][0], c + velocities[i][1], e)
     ]
-    for e in offsets
+    for e in offsets + far
+}
+shares_of = {
+    e: [(x, y) for x in (-1, 0, 1) for y in range(-1, ROWS + 1) if in_halo(x, y, e)]
+    for e in offsets + far
 }
 start_of, total = {}, 0
-for e in offsets:
+for e in offsets + far:
     start_of[e] = total
-    total += len(pops_of[e])
+    total += len(pops_of[e]) + len(shares_of[e])
 TOTAL = total
 
 
@@ -164,13 +174,13 @@
 def kernel(
     sizes,
     scatter_hbm, speed_hbm, bubble_hbm, wall_hbm,
-    density_out, velocity_out,
+    fields_out,
     scatter, speed, bubble, wall,
     in_send, in_recv, out_send, out_recv,
-    psi, psi_x, psi_rest,
-    pops, solids,
+    edge_send, edge_x, edge_rest,
+    pops, psi, solids,
     send, recv,
-    load_sem, in_sems, out_sems, psi_sems, round_sems,
+    load_sem, in_sems, out_sems, edge_sems, round_sems,
 ):
     nx, ny, nz = sizes
     gx, gy, gz = lax.axis_index("gx"), lax.axis_index("gy"), lax.axis_index("gz")
@@ -195,7 +205,7 @@
     for load in loads:
         load.start()
     barrier = pltpu.get_barrier_semaphore()
-    where_to = [neighbour(e) for e in offsets]
+    where_to = [neighbour(e) for e in offsets + far]
     peers = [lax.rem(gz + k, nz) for k in range(1, nz)]
     for target in where_to + [{"gx": gx, "gy": gy, "gz": peer} for peer in peers]:
         pl.semaphore_signal(barrier, inc=1, device_id=target, device_id_type=MESH)
@@ -236,9 +246,41 @@
         return in_recv[pl.ds(field * ROWS + c, 8, stride=IN_ROWS), :]
 
     for c in range(ROWS):
-        solids[c] = line(4, c)
+        solid = line(4, c)
+        solids[1, c + 1] = solid
+        edge_send[c, 0] = jnp.where(solid > 0.5, 0.5, pseudo_potential(line(0, c)))
+        edge_send[c, 1] = solid
+    copies = []
+    for k, e in enumerate(offsets):
+        if e[1] == 0:
+            source, target = edge_send, edge_x.at[k]
+        else:
+            source, target = edge_send.at[ROWS - 1 if e[1] > 0 else 0], edge_rest.at[k - 2]
+        copies.append(
+            pltpu.make_async_remote_copy(
+                src_ref=source,
+                dst_ref=target,
+                send_sem=edge_sems.at[0, k],
+                recv_sem=edge_sems.at[1, k],
+                device_id=where_to[k],
+                device_id_type=MESH,
+            )
+        )
+        copies[-1].start()
+    for c in range(ROWS):
         for i, value in enumerate(equilibrium(line(0, c), (line(1, c), line(2, c), line(3, c)))):
             pops[0, i, c] = value
+    for copy in copies:
+        copy.wait()
+    for k, e in enumerate(offsets):
+        if e[1] == 0:
+            for c in range(ROWS):
+                psi[1 - e[0], c + 1] = edge_x[k, c, 0]
+                solids[1 - e[0], c + 1] = edge_x[k, c, 1]
+        else:
+            y = 0 if e[1] > 0 else ROWS + 1
+            psi[1 - e[0], y] = edge_rest[k - 2, 0]
+            solids[1 - e[0], y] = edge_rest[k - 2, 1]
 
     lane = lax.broadcasted_iota(jnp.int32, (8, 128), 1)
     is_first, is_last = lane == 0, lane == 127
@@ -248,37 +290,18 @@
         carried = pltpu.roll(rolled, 1 if by > 0 else 7, 0)
         return jnp.where(is_first if by > 0 else is_last, carried, rolled)
 
-    def step(r, now, later):
+    halo = [(x, y) for x in (-1, 0, 1) for y in range(-1, ROWS + 1) if in_halo(x, y, (0, 0))]
+
+    def at(x, y):
+        return psi[x + 1, y + 1]
+
+    def potential_of(x, y, rho):
+        psi[x + 1, y + 1] = jnp.where(solids[x + 1, y + 1] > 0.5, 0.5, pseudo_potential(rho))
+
+    def step(r, now, later, last):
         for c in range(ROWS):
-            rho, _ = density_and_momentum([pops[now, i, c] for i in range(19)])
-            psi[r, c] = jnp.where(solids[c] > 0.5, 0.5, pseudo_potential(rho))
-        copies = []
-        for k, e in enumerate(offsets):
-            if e[1] == 0:
-                source, target = psi.at[r], psi_x.at[r, k]
-            else:
-                source, target = psi.at[r, ROWS - 1 if e[1] > 0 else 0], psi_rest.at[r, k - 2]
-            copies.append(
-                pltpu.make_async_remote_copy(
-                    src_ref=source,
-                    dst_ref=target,
-                    send_sem=psi_sems.at[0, r, k],
-                    recv_sem=psi_sems.at[1, r, k],
-                    device_id=where_to[k],
-                    device_id_type=MESH,
-                )
-            )
-            copies[-1].start()
-        for copy in copies:
-            copy.wait()
-
-        def at(x, y):
-            side = -1 if y < 0 else (1 if y >= ROWS else 0)
-            if (x, side) == (0, 0):
-                return psi[r, y]
-            k = offsets.index((-x, -side))
-            return psi_x[r, k, y] if side == 0 else psi_rest[r, k - 2]
-
+            potential_of(0, c, density_and_momentum([pops[now, i, c] for i in range(19)])[0])
+        share = {}
         for c in range(ROWS):
             here = at(0, c)
             spread = [at(1, y) - at(-1, y) for y in (c - 1, c, c + 1)]
@@ -290,18 +313,26 @@
                 scale * ((2.0 * middle + (left + right)) + (shift(middle, 1) + shift(middle, -1))),
                 scale * (shift(around, -1) - shift(around, 1)),
             )
-            post = collide([pops[now, i, c] for i in range(19)], force, solids[c] > 0.5)
+            post = collide([pops[now, i, c] for i in range(19)], force, solids[1, c + 1] > 0.5)
             for i, (cx, cy, cz) in enumerate(velocities):
                 value = shift(post[i], cz) if cz else post[i]
-                if in_block(cx, c + cy, (0, 0)):
+                node = cx, c + cy
+                if not last:
+                    share[node] = share[node] + value if node in share else value
+                if in_block(*node, (0, 0)):
                     pops[later, i, c + cy] = value
                 else:
                     for e in offsets:
-                        if in_block(cx, c + cy, e):
+                        if in_block(*node, e):
                             send[r, start_of[e] + pops_of[e].index((i, c))] = value
         copies = []
-        for k, e in enumerate(offsets):
+        for k, e in enumerate(offsets if last else offsets + far):
             part = pl.ds(start_of[e], len(pops_of[e]))
+            if not last:
+                first = start_of[e] + len(pops_of[e])
+                for n, node in enumerate(shares_of[e]):
+                    send[r, first + n] = share[node]
+                part = pl.ds(start_of[e], len(pops_of[e]) + len(shares_of[e]))
             copies.append(
                 pltpu.make_async_remote_copy(
                     src_ref=send.at[r, part],
@@ -318,17 +349,26 @@
         for e in offsets:
             for k, (i, c) in enumerate(pops_of[e]):
                 pops[later, i, c + velocities[i][1] - ROWS * e[1]] = recv[r, start_of[e] + k]
+        if not last:
+            for x, y in halo:
+                rho = share[x, y]
+                for e in offsets + far:
+                    there = (x + e[0], y + ROWS * e[1])
+                    if there in shares_of[e]:
+                        rho = rho + recv[r, start_of[e] + len(pops_of[e]) + shares_of[e].index(there)]
+                potential_of(x, y, rho)
 
     def body(r, carry):
         now = lax.rem(r, 2)
-        step(r, now, 1 - now)
+        step(r, now, 1 - now, False)
         return carry
 
-    lax.fori_loop(0, STEPS, body, 0)
+    lax.fori_loop(0, STEPS - 1, body, 0)
+    step(STEPS - 1, (STEPS - 1) % 2, STEPS % 2, True)
 
     for c in range(ROWS):
         rho, momentum = density_and_momentum([pops[STEPS % 2, i, c] for i in range(19)])
-        fluid = solids[c] < 0.5
+        fluid = solids[1, c + 1] < 0.5
         scale = math.sqrt(3.0) / rho
         fields = [rho * (1.0 / 0.28)] + [j * scale for j in momentum]
         for k, field in enumerate(fields):
@@ -338,9 +378,8 @@
         for half in range(2):
             first = (p * 2 + half) * OUT_ROWS
             rows = slice(half * ROWS, (half + 1) * ROWS)
-            density_out[p, rows, :] = out_recv[first : first + ROWS, :]
-            for k in range(3):
-                velocity_out[k, p, rows, :] = out_recv[first + (k + 1) * ROWS : first + (k + 2) * ROWS, :]
+            for k in range(4):
+                fields_out[k, p, rows, :] = out_recv[first + k * ROWS : first + (k + 1) * ROWS, :]
 
 
 def solution(mesh):
@@ -349,15 +388,11 @@
     tile = (8, 128)
 
     def on_device(density_scatter, initial_velocity, bubble_mask, wall_flags):
-        return tuple(
-            pl.pallas_call(
+        fields = pl.pallas_call(
                 functools.partial(kernel, sizes),
-                out_shape=[
-                    jax.ShapeDtypeStruct(block, jnp.float32),
-                    jax.ShapeDtypeStruct((3,) + block, jnp.float32),
-                ],
+                out_shape=jax.ShapeDtypeStruct((4,) + block, jnp.float32),
                 in_specs=[pl.BlockSpec(memory_space=pl.ANY)] * 4,
-                out_specs=[pl.BlockSpec(memory_space=pltpu.VMEM)] * 2,
+                out_specs=pl.BlockSpec(memory_space=pltpu.VMEM),
                 scratch_shapes=[
                     pltpu.VMEM(block, jnp.float32),
                     pltpu.VMEM((3,) + block, jnp.float32),
@@ -367,22 +402,23 @@
                     pltpu.VMEM((8 * IN_ROWS, 128), jnp.float32),
                     pltpu.VMEM((8 * OUT_ROWS, 128), jnp.float32),
                     pltpu.VMEM((8 * OUT_ROWS, 128), jnp.float32),
-                    pltpu.VMEM((STEPS, ROWS) + tile, jnp.float32),
-                    pltpu.VMEM((STEPS, 2, ROWS) + tile, jnp.float32),
-                    pltpu.VMEM((STEPS, 6) + tile, jnp.float32),
+                    pltpu.VMEM((ROWS, 2) + tile, jnp.float32),
+                    pltpu.VMEM((2, ROWS, 2) + tile, jnp.float32),
+                    pltpu.VMEM((6, 2) + tile, jnp.float32),
                     pltpu.VMEM((2, 19, ROWS) + tile, jnp.float32),
-                    pltpu.VMEM((ROWS,) + tile, jnp.float32),
+                    pltpu.VMEM((3, ROWS + 2) + tile, jnp.float32),
+                    pltpu.VMEM((3, ROWS + 2) + tile, jnp.float32),
                     pltpu.VMEM((STEPS, TOTAL) + tile, jnp.float32),
                     pltpu.VMEM((STEPS, TOTAL) + tile, jnp.float32),
                     pltpu.SemaphoreType.DMA((4,)),
                     pltpu.SemaphoreType.DMA((2, 7)),
                     pltpu.SemaphoreType.DMA((2, 7)),
-                    pltpu.SemaphoreType.DMA((2, STEPS, 8)),
-                    pltpu.SemaphoreType.DMA((2, STEPS, 8)),
+                    pltpu.SemaphoreType.DMA((2, 8)),
+                    pltpu.SemaphoreType.DMA((2, STEPS, 14)),
                 ],
                 compiler_params=pltpu.CompilerParams(collective_id=0, has_side_effects=True),
             )(density_scatter, initial_velocity, bubble_mask, wall_flags)
-        )
+        return fields[0], fields[1:]
 
     return jax.shard_map(
         on_device,

time: 78.8 us -> 70.1 us (0.89)
  Pallas kernels: 75 us -> 66.3 us
    pallas_call x1, Pallas kernels: 75 us -> 66.3 us  [on_device(): pl.pallas_call(functools.partial(kernel, sizes), out_shape=jax.ShapeDtype...]
    unnamed x2 -> x0, local copies, waits for them, and re-layouts: 2.74 us -> none
    slice x0 -> x1, local copies, waits for them, and re-layouts: none -> 1.42 us  [on_device(): return (fields[0], fields[1:])]
    squeeze x0 -> x1, local copies, waits for them, and re-layouts: none -> 1.32 us  [on_device(): return (fields[0], fields[1:])]
where the time goes in v2:
time: 70.1 us; the launch traced here: 69.7 us
  Pallas kernels  66.3 us (95%)
  local copies, waits for them, and re-layouts  2.74 us (4%)
    pallas_call x1, Pallas kernels, on_device(): pl.pallas_call(functools.partial(kernel, sizes), out_shape=jax.ShapeDtype...  66.3 us
    slice x1, local copies, waits for them, and re-layouts, on_device(): return (fields[0], fields[1:])  1.42 us

profile of v2, /device:TPU:1, one launch (start us, length us, event | category | flops | bytes accessed | tf_op | source)
XLA Modules:
  0.0 69.7 jit_solution(11127803841163483662)
XLA Ops:
  0.6 66.3 %shard_map.59 = f32[4,4,8,128]{3,2,1,0:T(8,128)} custom-call(f32[4,8,128]{2,1,0:T(8,128)} %scatter_hbm.1, f32[3,4,8,128]{3,2,1,0:T(8,128)} %speed_hbm.1, s32[4,8,128]{2,1,0:T(8,128)} %bubble_hbm.1, s32[4,8,128]{2,1,0:T(8,128)} %wall_hbm.1), custom_call_target="tpu_custom_call" | custom-call | tf_op jit(solution)/shard_map/pallas_call | solution.py:391
  66.9 1.3 %slice_bitcast_fusion = f32[4,8,128]{2,1,0:T(8,128)} fusion(f32[4,4,8,128]{3,2,1,0:T(8,128)} %shard_map.59), kind=kLoop, calls=%fused_computation | loop fusion | bytes 32768 | tf_op jit(solution)/shard_map/squeeze | solution.py:421
  68.3 1.4 %slice.7 = f32[3,4,8,128]{3,2,1,0:T(8,128)} slice(f32[4,4,8,128]{3,2,1,0:T(8,128)} %shard_map.59), slice={[1:4], [0:4], [0:8], [0:128]} | slice | bytes 98304 | tf_op jit(solution)/shard_map/slice | solution.py:421

commit v3 on v2

--- a/solution.py
+++ b/solution.py
@@ -176,11 +176,11 @@
     scatter_hbm, speed_hbm, bubble_hbm, wall_hbm,
     fields_out,
     scatter, speed, bubble, wall,
-    in_send, in_recv, out_send, out_recv,
+    in_send, in_recv, out_send,
     edge_send, edge_x, edge_rest,
     pops, psi, solids,
     send, recv,
-    load_sem, in_sems, out_sems, edge_sems, round_sems,
+    load_sem, own_sem, in_sems, out_sems, edge_sems, round_sems,
 ):
     nx, ny, nz = sizes
     gx, gy, gz = lax.axis_index("gx"), lax.axis_index("gy"), lax.axis_index("gz")
@@ -207,7 +207,7 @@
     barrier = pltpu.get_barrier_semaphore()
     where_to = [neighbour(e) for e in offsets + far]
     peers = [lax.rem(gz + k, nz) for k in range(1, nz)]
-    for target in where_to + [{"gx": gx, "gy": gy, "gz": peer} for peer in peers]:
+    for target in where_to[: len(offsets)] + [{"gx": gx, "gy": gy, "gz": peer} for peer in peers]:
         pl.semaphore_signal(barrier, inc=1, device_id=target, device_id_type=MESH)
     for load in loads:
         load.wait()
@@ -220,7 +220,7 @@
             first = (p * 2 + half) * IN_ROWS
             for k, field in enumerate(fields):
                 in_send[first + k * ROWS : first + (k + 1) * ROWS, :] = field[half * ROWS : (half + 1) * ROWS]
-    pl.semaphore_wait(barrier, len(where_to) + len(peers))
+    pl.semaphore_wait(barrier, len(offsets) + len(peers))
 
     def exchange(source, target, rows, sems):
         mine = pl.ds(pl.multiple_of(gz * rows, 8), rows)
@@ -236,9 +236,11 @@
             )
             copy.start()
             copies.append(copy)
-        target[mine, :] = source[mine, :]
+        own = pltpu.make_async_copy(source.at[mine, :], target.at[mine, :], own_sem)
+        own.start()
         for copy in copies:
             copy.wait()
+        own.wait()
 
     exchange(in_send, in_recv, IN_ROWS, in_sems)
 
@@ -251,7 +253,7 @@
         edge_send[c, 0] = jnp.where(solid > 0.5, 0.5, pseudo_potential(line(0, c)))
         edge_send[c, 1] = solid
     copies = []
-    for k, e in enumerate(offsets):
+    for k, e in reversed(list(enumerate(offsets))):
         if e[1] == 0:
             source, target = edge_send, edge_x.at[k]
         else:
@@ -301,6 +303,22 @@
     def step(r, now, later, last):
         for c in range(ROWS):
             potential_of(0, c, density_and_momentum([pops[now, i, c] for i in range(19)])[0])
+        copies = []
+
+        def launch(e, k, first, count):
+            part = pl.ds(first, count)
+            copies.append(
+                pltpu.make_async_remote_copy(
+                    src_ref=send.at[r, part],
+                    dst_ref=recv.at[r, part],
+                    send_sem=round_sems.at[0, r, k],
+                    recv_sem=round_sems.at[1, r, k],
+                    device_id=where_to[(offsets + far).index(e)],
+                    device_id_type=MESH,
+                )
+            )
+            copies[-1].start()
+
         share = {}
         for c in range(ROWS):
             here = at(0, c)
@@ -325,25 +343,13 @@
                     for e in offsets:
                         if in_block(*node, e):
                             send[r, start_of[e] + pops_of[e].index((i, c))] = value
-        copies = []
-        for k, e in enumerate(offsets if last else offsets + far):
-            part = pl.ds(start_of[e], len(pops_of[e]))
+        for k, e in reversed(list(enumerate(offsets if last else offsets + far))):
+            first, count = start_of[e], len(pops_of[e])
             if not last:
-                first = start_of[e] + len(pops_of[e])
                 for n, node in enumerate(shares_of[e]):
-                    send[r, first + n] = share[node]
-                part = pl.ds(start_of[e], len(pops_of[e]) + len(shares_of[e]))
-            copies.append(
-                pltpu.make_async_remote_copy(
-                    src_ref=send.at[r, part],
-                    dst_ref=recv.at[r, part],
-                    send_sem=round_sems.at[0, r, k],
-                    recv_sem=round_sems.at[1, r, k],
-                    device_id=where_to[k],
-                    device_id_type=MESH,
-                )
-            )
-            copies[-1].start()
+                    send[r, start_of[e] + len(pops_of[e]) + n] = share[node]
+                count += len(shares_of[e])
+            launch(e, k, first, count)
         for copy in copies:
             copy.wait()
         for e in offsets:
@@ -373,13 +379,17 @@
         fields = [rho * (1.0 / 0.28)] + [j * scale for j in momentum]
         for k, field in enumerate(fields):
             out_send[pl.ds(k * ROWS + c, 8, stride=OUT_ROWS), :] = jnp.where(fluid, field, 0.0)
-    exchange(out_send, out_recv, OUT_ROWS, out_sems)
+    exchange(out_send, fields_out, OUT_ROWS, out_sems)
+
+
+def unpack(fields, density_out, velocity_out):
     for p in range(4):
         for half in range(2):
             first = (p * 2 + half) * OUT_ROWS
             rows = slice(half * ROWS, (half + 1) * ROWS)
-            for k in range(4):
-                fields_out[k, p, rows, :] = out_recv[first + k * ROWS : first + (k + 1) * ROWS, :]
+            density_out[p, rows, :] = fields[first : first + ROWS, :]
+            for k in range(3):
+                velocity_out[k, p, rows, :] = fields[first + (k + 1) * ROWS : first + (k + 2) * ROWS, :]
 
 
 def solution(mesh):
@@ -390,9 +400,9 @@
     def on_device(density_scatter, initial_velocity, bubble_mask, wall_flags):
         fields = pl.pallas_call(
                 functools.partial(kernel, sizes),
-                out_shape=jax.ShapeDtypeStruct((4,) + block, jnp.float32),
+                out_shape=jax.ShapeDtypeStruct((8 * OUT_ROWS, 128), jnp.float32),
                 in_specs=[pl.BlockSpec(memory_space=pl.ANY)] * 4,
-                out_specs=pl.BlockSpec(memory_space=pltpu.VMEM),
+                out_specs=pl.BlockSpec(memory_space=pl.ANY),
                 scratch_shapes=[
                     pltpu.VMEM(block, jnp.float32),
                     pltpu.VMEM((3,) + block, jnp.float32),
@@ -400,7 +410,6 @@
                     pltpu.VMEM(block, jnp.int32),
                     pltpu.VMEM((8 * IN_ROWS, 128), jnp.float32),
                     pltpu.VMEM((8 * IN_ROWS, 128), jnp.float32),
-                    pltpu.VMEM((8 * OUT_ROWS, 128), jnp.float32),
                     pltpu.VMEM((8 * OUT_ROWS, 128), jnp.float32),
                     pltpu.VMEM((ROWS, 2) + tile, jnp.float32),
                     pltpu.VMEM((2, ROWS, 2) + tile, jnp.float32),
@@ -411,6 +420,7 @@
                     pltpu.VMEM((STEPS, TOTAL) + tile, jnp.float32),
                     pltpu.VMEM((STEPS, TOTAL) + tile, jnp.float32),
                     pltpu.SemaphoreType.DMA((4,)),
+                    pltpu.SemaphoreType.DMA,
                     pltpu.SemaphoreType.DMA((2, 7)),
                     pltpu.SemaphoreType.DMA((2, 7)),
                     pltpu.SemaphoreType.DMA((2, 8)),
@@ -418,7 +428,17 @@
                 ],
                 compiler_params=pltpu.CompilerParams(collective_id=0, has_side_effects=True),
             )(density_scatter, initial_velocity, bubble_mask, wall_flags)
-        return fields[0], fields[1:]
+        return tuple(
+            pl.pallas_call(
+                unpack,
+                out_shape=[
+                    jax.ShapeDtypeStruct(block, jnp.float32),
+                    jax.ShapeDtypeStruct((3,) + block, jnp.float32),
+                ],
+                in_specs=[pl.BlockSpec(memory_space=pltpu.VMEM)],
+                out_specs=[pl.BlockSpec(memory_space=pltpu.VMEM)] * 2,
+            )(fields)
+        )
 
     return jax.shard_map(
         on_device,

time: 70.1 us -> 64.4 us (0.919)
  Pallas kernels: 66.3 us -> 63.5 us
  local copies, waits for them, and re-layouts: 2.74 us -> 0 us
    pallas_call x1, Pallas kernels: 66.3 us -> 62 us  [on_device(): pl.pallas_call(functools.partial(kernel, sizes), out_shape=jax.ShapeDtype...]
    pallas_call x0 -> x1, Pallas kernels: none -> 1.48 us  [on_device(): pl.pallas_call(unpack, out_shape=[jax.ShapeDtypeStruct(block, jnp.float32...]
    slice x1 -> x0, local copies, waits for them, and re-layouts: 1.42 us -> none  [on_device(): return (fields[0], fields[1:])]
    squeeze x1 -> x0, local copies, waits for them, and re-layouts: 1.32 us -> none  [on_device(): return (fields[0], fields[1:])]
where the time goes in v3:
time: 64.4 us; the launch traced here: 64.1 us
  Pallas kernels  63.5 us (99%)
    pallas_call x1, Pallas kernels, on_device(): pl.pallas_call(functools.partial(kernel, sizes), out_shape=jax.ShapeDtype...  62 us
    pallas_call x1, Pallas kernels, on_device(): pl.pallas_call(unpack, out_shape=[jax.ShapeDtypeStruct(block, jnp.float32...  1.48 us

profile of v3, /device:TPU:1, one launch (start us, length us, event | category | flops | bytes accessed | tf_op | source)
XLA Modules:
  0.0 64.1 jit_solution(10555449667263786843)
XLA Ops:
  0.6 62.0 %shard_map.59.fields = f32[128,128]{1,0:T(8,128)} custom-call(f32[4,8,128]{2,1,0:T(8,128)} %scatter_hbm.1, f32[3,4,8,128]{3,2,1,0:T(8,128)} %speed_hbm.1, s32[4,8,128]{2,1,0:T(8,128)} %bubble_hbm.1, s32[4,8,128]{2,1,0:T(8,128)} %wall_hbm.1), custom_call_target="tpu_custom_call" | custom-call | tf_op jit(solution)/shard_map/pallas_call | solution.py:401
  62.6 1.5 %shard_map.60 = (f32[4,8,128]{2,1,0:T(8,128)}, f32[3,4,8,128]{3,2,1,0:T(8,128)}) custom-call(f32[128,128]{1,0:T(8,128)} %shard_map.59.fields), custom_call_target="tpu_custom_call" | custom-call | tf_op jit(solution)/shard_map/pallas_call | solution.py:432

commit v4 on v3

--- a/solution.py
+++ b/solution.py
@@ -19,7 +19,8 @@
 ]
 opposite = [0, 2, 1, 4, 3, 6, 5, 8, 7, 10, 9, 12, 11, 14, 13, 16, 15, 18, 17]
 ROWS = 4
-IN_ROWS = 24
+FIRST_ROWS = 8
+NEXT_ROWS = 16
 OUT_ROWS = 16
 
 offsets = [(1, 0), (-1, 0), (0, 1), (0, -1), (1, 1), (1, -1), (-1, 1), (-1, -1)]
@@ -176,7 +177,7 @@
     scatter_hbm, speed_hbm, bubble_hbm, wall_hbm,
     fields_out,
     scatter, speed, bubble, wall,
-    in_send, in_recv, out_send,
+    first_send, first_recv, next_send, next_recv, out_send,
     edge_send, edge_x, edge_rest,
     pops, psi, solids,
     send, recv,
@@ -206,7 +207,11 @@
         load.start()
     barrier = pltpu.get_barrier_semaphore()
     where_to = [neighbour(e) for e in offsets + far]
-    peers = [lax.rem(gz + k, nz) for k in range(1, nz)]
+    bits = [lax.rem(gz, 2), lax.rem(lax.div(gz, 2), 2), lax.div(gz, 4)]
+    peers = [
+        sum((1 - bit if k & (1 << n) else bit) * (1 << n) for n, bit in enumerate(bits))
+        for k in range(7, 0, -1)
+    ]
     for target in where_to[: len(offsets)] + [{"gx": gx, "gy": gy, "gz": peer} for peer in peers]:
         pl.semaphore_signal(barrier, inc=1, device_id=target, device_id_type=MESH)
     for load in loads:
@@ -215,42 +220,49 @@
     for p in range(4):
         rho0 = jnp.where(bubble[p] == 1, 0.06, 0.28) * scatter[p]
         solid = jnp.where(wall[p] == 1, 1.0, 0.0)
-        fields = [rho0, speed[0, p], speed[1, p], speed[2, p], solid]
         for half in range(2):
-            first = (p * 2 + half) * IN_ROWS
-            for k, field in enumerate(fields):
-                in_send[first + k * ROWS : first + (k + 1) * ROWS, :] = field[half * ROWS : (half + 1) * ROWS]
+            rows = slice(half * ROWS, (half + 1) * ROWS)
+            for packed, size, group in (
+                (first_send, FIRST_ROWS, (rho0, solid)),
+                (next_send, NEXT_ROWS, (speed[0, p], speed[1, p], speed[2, p])),
+            ):
+                first = (p * 2 + half) * size
+                for k, field in enumerate(group):
+                    packed[first + k * ROWS : first + (k + 1) * ROWS, :] = field[rows]
     pl.semaphore_wait(barrier, len(offsets) + len(peers))
 
-    def exchange(source, target, rows, sems):
+    def exchange(source, target, rows, sems, own_sem):
         mine = pl.ds(pl.multiple_of(gz * rows, 8), rows)
         copies = []
         for k, peer in enumerate(peers):
-            copy = pltpu.make_async_remote_copy(
-                src_ref=source.at[pl.ds(pl.multiple_of(peer * rows, 8), rows), :],
-                dst_ref=target.at[mine, :],
-                send_sem=sems.at[0, k],
-                recv_sem=sems.at[1, k],
-                device_id={"gx": gx, "gy": gy, "gz": peer},
-                device_id_type=MESH,
+            copies.append(
+                pltpu.make_async_remote_copy(
+                    src_ref=source.at[pl.ds(pl.multiple_of(peer * rows, 8), rows), :],
+                    dst_ref=target.at[mine, :],
+                    send_sem=sems.at[0, k],
+                    recv_sem=sems.at[1, k],
+                    device_id={"gx": gx, "gy": gy, "gz": peer},
+                    device_id_type=MESH,
+                )
             )
-            copy.start()
-            copies.append(copy)
-        own = pltpu.make_async_copy(source.at[mine, :], target.at[mine, :], own_sem)
-        own.start()
-        for copy in copies:
-            copy.wait()
-        own.wait()
-
-    exchange(in_send, in_recv, IN_ROWS, in_sems)
-
-    def line(field, c):
-        return in_recv[pl.ds(field * ROWS + c, 8, stride=IN_ROWS), :]
+            copies[-1].start()
+        copies.append(pltpu.make_async_copy(source.at[mine, :], target.at[mine, :], own_sem))
+        copies[-1].start()
+        return copies
+
+    first_copies = exchange(first_send, first_recv, FIRST_ROWS, in_sems.at[0], own_sem.at[0])
+    next_copies = exchange(next_send, next_recv, NEXT_ROWS, in_sems.at[1], own_sem.at[1])
+    for copy in first_copies:
+        copy.wait()
+
+    def line(packed, rows, field, c):
+        return packed[pl.ds(field * ROWS + c, 8, stride=rows), :]
 
     for c in range(ROWS):
-        solid = line(4, c)
+        solid = line(first_recv, FIRST_ROWS, 1, c)
+        rho0 = line(first_recv, FIRST_ROWS, 0, c)
         solids[1, c + 1] = solid
-        edge_send[c, 0] = jnp.where(solid > 0.5, 0.5, pseudo_potential(line(0, c)))
+        edge_send[c, 0] = jnp.where(solid > 0.5, 0.5, pseudo_potential(rho0))
         edge_send[c, 1] = solid
     copies = []
     for k, e in reversed(list(enumerate(offsets))):
@@ -269,8 +281,12 @@
             )
         )
         copies[-1].start()
+    for copy in next_copies:
+        copy.wait()
     for c in range(ROWS):
-        for i, value in enumerate(equilibrium(line(0, c), (line(1, c), line(2, c), line(3, c)))):
+        rho0 = line(first_recv, FIRST_ROWS, 0, c)
+        speed0 = [line(next_recv, NEXT_ROWS, k, c) for k in range(3)]
+        for i, value in enumerate(equilibrium(rho0, speed0)):
             pops[0, i, c] = value
     for copy in copies:
         copy.wait()
@@ -379,7 +395,8 @@
         fields = [rho * (1.0 / 0.28)] + [j * scale for j in momentum]
         for k, field in enumerate(fields):
             out_send[pl.ds(k * ROWS + c, 8, stride=OUT_ROWS), :] = jnp.where(fluid, field, 0.0)
-    exchange(out_send, fields_out, OUT_ROWS, out_sems)
+    for copy in exchange(out_send, fields_out, OUT_ROWS, out_sems, own_sem.at[2]):
+        copy.wait()
 
 
 def unpack(fields, density_out, velocity_out):
@@ -408,8 +425,10 @@
                     pltpu.VMEM((3,) + block, jnp.float32),
                     pltpu.VMEM(block, jnp.int32),
                     pltpu.VMEM(block, jnp.int32),
-                    pltpu.VMEM((8 * IN_ROWS, 128), jnp.float32),
-                    pltpu.VMEM((8 * IN_ROWS, 128), jnp.float32),
+                    pltpu.VMEM((8 * FIRST_ROWS, 128), jnp.float32),
+                    pltpu.VMEM((8 * FIRST_ROWS, 128), jnp.float32),
+                    pltpu.VMEM((8 * NEXT_ROWS, 128), jnp.float32),
+                    pltpu.VMEM((8 * NEXT_ROWS, 128), jnp.float32),
                     pltpu.VMEM((8 * OUT_ROWS, 128), jnp.float32),
                     pltpu.VMEM((ROWS, 2) + tile, jnp.float32),
                     pltpu.VMEM((2, ROWS, 2) + tile, jnp.float32),
@@ -420,8 +439,8 @@
                     pltpu.VMEM((STEPS, TOTAL) + tile, jnp.float32),
                     pltpu.VMEM((STEPS, TOTAL) + tile, jnp.float32),
                     pltpu.SemaphoreType.DMA((4,)),
-                    pltpu.SemaphoreType.DMA,
-                    pltpu.SemaphoreType.DMA((2, 7)),
+                    pltpu.SemaphoreType.DMA((3,)),
+                    pltpu.SemaphoreType.DMA((2, 2, 7)),
                     pltpu.SemaphoreType.DMA((2, 7)),
                     pltpu.SemaphoreType.DMA((2, 8)),
                     pltpu.SemaphoreType.DMA((2, STEPS, 14)),

time: 64.4 us -> 64.2 us (level)
  no operation moved by 1% of the time
where the time goes in v4:
time: 64.2 us; the launch traced here: 63.7 us
  Pallas kernels  63.1 us (98%)
    pallas_call x1, Pallas kernels, on_device(): pl.pallas_call(functools.partial(kernel, sizes), out_shape=jax.ShapeDtype...  61.6 us
    pallas_call x1, Pallas kernels, on_device(): pl.pallas_call(unpack, out_shape=[jax.ShapeDtypeStruct(block, jnp.float32...  1.48 us

profile of v4, /device:TPU:1, one launch (start us, length us, event | category | flops | bytes accessed | tf_op | source)
XLA Modules:
  0.0 63.7 jit_solution(14899804912392681515)
XLA Ops:
  0.6 61.6 %shard_map.59.fields = f32[128,128]{1,0:T(8,128)} custom-call(f32[4,8,128]{2,1,0:T(8,128)} %scatter_hbm.1, f32[3,4,8,128]{3,2,1,0:T(8,128)} %speed_hbm.1, s32[4,8,128]{2,1,0:T(8,128)} %bubble_hbm.1, s32[4,8,128]{2,1,0:T(8,128)} %wall_hbm.1), custom_call_target="tpu_custom_call" | custom-call | tf_op jit(solution)/shard_map/pallas_call | solution.py:418
  62.2 1.5 %shard_map.60 = (f32[4,8,128]{2,1,0:T(8,128)}, f32[3,4,8,128]{3,2,1,0:T(8,128)}) custom-call(f32[128,128]{1,0:T(8,128)} %shard_map.59.fields), custom_call_target="tpu_custom_call" | custom-call | tf_op jit(solution)/shard_map/pallas_call | solution.py:451

commit v5 on v4

--- a/solution.py
+++ b/solution.py
@@ -418,8 +418,8 @@
         fields = pl.pallas_call(
                 functools.partial(kernel, sizes),
                 out_shape=jax.ShapeDtypeStruct((8 * OUT_ROWS, 128), jnp.float32),
-                in_specs=[pl.BlockSpec(memory_space=pl.ANY)] * 4,
-                out_specs=pl.BlockSpec(memory_space=pl.ANY),
+                in_specs=[pl.BlockSpec(memory_space=pltpu.HBM)] * 4,
+                out_specs=pl.BlockSpec(memory_space=pltpu.VMEM),
                 scratch_shapes=[
                     pltpu.VMEM(block, jnp.float32),
                     pltpu.VMEM((3,) + block, jnp.float32),
@@ -445,8 +445,8 @@
                     pltpu.SemaphoreType.DMA((2, 8)),
                     pltpu.SemaphoreType.DMA((2, STEPS, 14)),
                 ],
-                compiler_params=pltpu.CompilerParams(collective_id=0, has_side_effects=True),
-            )(density_scatter, initial_velocity, bubble_mask, wall_flags)
+                compiler_params=pltpu.CompilerParams(collective_id=0, has_side_effects=True, vmem_limit_bytes=16 << 20),
+            )(*(pltpu.with_memory_space_constraint(a, pltpu.HBM) for a in (density_scatter, initial_velocity, bubble_mask, wall_flags)))
         return tuple(
             pl.pallas_call(
                 unpack,
@@ -456,6 +456,7 @@
                 ],
                 in_specs=[pl.BlockSpec(memory_space=pltpu.VMEM)],
                 out_specs=[pl.BlockSpec(memory_space=pltpu.VMEM)] * 2,
+                compiler_params=pltpu.CompilerParams(vmem_limit_bytes=4 << 20),
             )(fields)
         )
 

time: 64.2 us -> 63.1 us (0.983)
  Pallas kernels: 63.1 us -> 62.1 us
    pallas_call x1, Pallas kernels: 1.48 us -> 0.64 us  [on_device(): pl.pallas_call(unpack, out_shape=[jax.ShapeDtypeStruct(block, jnp.float32...]
where the time goes in v5:
time: 63.1 us; the launch traced here: 62.7 us
  Pallas kernels  62.1 us (98%)
  between operations  0.64 us (1%)
    pallas_call x1, Pallas kernels, on_device(): pl.pallas_call(functools.partial(kernel, sizes), out_shape=jax.ShapeDtype...  61.5 us

profile of v5, /device:TPU:1, one launch (start us, length us, event | category | flops | bytes accessed | tf_op | source)
XLA Modules:
  0.0 62.7 jit_solution(3275398333540567550)
XLA Ops:
  0.6 61.5 %shard_map.59.fields = f32[128,128]{1,0:T(8,128)S(1)} custom-call(f32[4,8,128]{2,1,0:T(8,128)} %scatter_hbm.1, f32[3,4,8,128]{3,2,1,0:T(8,128)} %speed_hbm.1, s32[4,8,128]{2,1,0:T(8,128)} %bubble_hbm.1, s32[4,8,128]{2,1,0:T(8,128)} %wall_hbm.1), custom_call_target="tpu_custom_call" | custom-call | tf_op jit(solution)/shard_map/pallas_call | solution.py:418
  62.1 0.6 %shard_map.60 = (f32[4,8,128]{2,1,0:T(8,128)}, f32[3,4,8,128]{3,2,1,0:T(8,128)}) custom-call(f32[128,128]{1,0:T(8,128)S(1)} %shard_map.59.fields), custom_call_target="tpu_custom_call" | custom-call | tf_op jit(solution)/shard_map/pallas_call | solution.py:451
